TPU v7x, 16 devices: a 4x2x1 block of a 4x4x8 slice. The times are simulated.
16 devices in a mesh: dp: 2 (over y, z), tp: 8 (over x, core).
Axes of the slice: x: 4, y: 2, z: 1, core: 2. Of those that a mesh axis runs over, the one named last changes fastest.
The devices are a block of a 4x4x8 slice.
Arguments:
- hidden: bfloat16 [1536, 896], P('dp'), parts along dimension 0
- tokens: int32 [1536], P('dp'), parts along dimension 0
- embedding: bfloat16 [151936, 896], P('tp')
- head_w: bfloat16 [896, 151936], P(None, 'tp')
- h_norm: float32 [896], replicated
- e_norm: float32 [896], replicated
- f_norm: float32 [896], replicated
- o_norm: float32 [896], replicated
- proj_w: bfloat16 [1792, 896], P(None, 'tp')
- w_gate: bfloat16 [896, 4864], P(None, 'tp')
- w_up: bfloat16 [896, 4864], P(None, 'tp')
- w_down: bfloat16 [4864, 896], P('tp')
Outputs:
- output 1: bfloat16 [1536, 896], P('dp'), parts along dimension 0
- output 2: float32 [1536, 151936], P('dp', 'tp'), parts along dimension 0
There are 2 independent parts. A program takes and returns all parts, laid end to end along the dimension named above; an argument that names none is the same for every part.
All inputs are finite; a program needn't handle non-finite values.
Results may differ from a plain program's by a relative error of at most 0.0110913.
Values are sent between devices in bfloat16 or wider.
A program may use at most 768 MiB of HBM per device.

v0:
```python
import jax
import jax.numpy as jnp
from jax import lax
from jax.sharding import PartitionSpec as P

NORM_EPS = 1e-6


def rms_norm(values, norm_gain):
    wide_vals = values.astype(jnp.float32)
    inv_rms = lax.rsqrt(jnp.mean(wide_vals * wide_vals, axis=-1, keepdims=True) + NORM_EPS)
    return wide_vals * inv_rms * norm_gain


def solution(mesh):
    def draft_step(hidden, tokens, embedding, head_w, h_norm, e_norm, f_norm, o_norm, proj_w, w_gate, w_up, w_down):
        tp_index = lax.axis_index("tp")
        vocab_local = embedding.shape[0]
        local_ids = tokens - tp_index * vocab_local
        owned_mask = (local_ids >= 0) & (local_ids < vocab_local)
        picked = jnp.take(embedding, jnp.clip(local_ids, 0, vocab_local - 1), axis=0)
        picked = jnp.where(owned_mask[:, None], picked, jnp.zeros_like(picked))
        emb_rows = lax.psum(picked, "tp")
        joined = jnp.concatenate([rms_norm(hidden, h_norm), rms_norm(emb_rows, e_norm)], axis=-1).astype(jnp.bfloat16)
        proj_cols = jnp.dot(joined, proj_w, preferred_element_type=jnp.float32).astype(jnp.bfloat16)
        proj_full = lax.all_gather(proj_cols, "tp", axis=1, tiled=True)
        normed = rms_norm(proj_full, f_norm).astype(jnp.bfloat16)
        gate_val = jnp.dot(normed, w_gate, preferred_element_type=jnp.float32)
        up_val = jnp.dot(normed, w_up, preferred_element_type=jnp.float32)
        act_val = (jax.nn.silu(gate_val) * up_val).astype(jnp.bfloat16)
        down_part = jnp.dot(act_val, w_down, preferred_element_type=jnp.float32)
        down_sum = lax.psum(down_part, "tp")
        new_u = (proj_full.astype(jnp.float32) + down_sum).astype(jnp.bfloat16)
        out_norm = rms_norm(new_u, o_norm).astype(jnp.bfloat16)
        logits = jnp.dot(out_norm, head_w, preferred_element_type=jnp.float32)
        row_max = lax.pmax(jnp.max(logits, axis=-1), "tp")
        shifted = logits - row_max[:, None]
        row_sum = lax.psum(jnp.sum(jnp.exp(shifted), axis=-1), "tp")
        return new_u, shifted - jnp.log(row_sum)[:, None]

    specs_in = (P("dp", None), P("dp"), P("tp", None), P(None, "tp"), P(None), P(None), P(None), P(None), P(None, "tp"), P(None, "tp"), P(None, "tp"), P("tp", None))
    specs_out = (P("dp", None), P("dp", "tp"))
    return jax.shard_map(draft_step, mesh=mesh, in_specs=specs_in, out_specs=specs_out, check_vma=False)
```

profile of v0, /device:TPU:113, one launch (start us, length us, event | category | flops | bytes accessed | tf_op | source)
XLA Modules:
  0.0 330.1 jit_solution(15257222399931021296)
XLA Ops:
  7.2 0.0 copy-start
  7.2 0.1 all-reduce.3.cloned.1.call-start
  7.3 0.8 compare_and_fusion
  8.0 21.6 %gather_fusion = bf16[768,896]{1,0:T(8,128)(2,1)} fusion(bf16[18992,896]{1,0:T(8,128)(2,1)} %param.14, s32[1024]{0:T(1024)S(1)} %pad_clamp_fusion), kind=kCustom, calls=%fused_computation | custom fusion | bytes 2755584 | tf_op jit(solution)/shard_map/jit(_take)/gather | solution.py:21
  29.6 0.0 copy-start.2
  29.6 2.9 select_select_fusion
  32.5 0.0 copy-start.7
  32.5 0.1 all-reduce.3.cloned.1.call-update
  32.6 0.1 all-gather.2.cloned.1.call-start
  32.6 0.0 copy-done.2
  32.7 0.3 fusion
  33.0 0.2 copy-done.7
  33.2 0.0 copy-start.8
  33.2 1.5 fusion.2
  34.7 59.8 %all-reduce.3.cloned.1.call-done = bf16[768,896]{1,0:T(8,128)(2,1)} async-done(((bf16[768,896]{1,0:T(8,128)(2,1)}), bf16[768,896]{1,0:T(8,128)(2,1)}) %all-reduce.3.cloned.1.call-update) | async-done | bytes 1376272 | tf_op jit(solution)/shard_map/psum | solution.py:23
  94.5 0.0 copy-start.4
  94.5 0.0 copy-start.6
  94.5 0.0 copy-start.9
  94.5 1.8 fusion.3
  96.4 0.0 copy-done.8
  96.4 0.0 copy-done.4
  96.4 0.4 fusion.5
  96.8 0.0 copy-done.6
  96.8 0.0 copy-done.9
  96.8 0.0 copy-start.10
  96.8 1.7 fusion.22
  98.5 0.1 all-gather.2.cloned.1.call-update
  98.5 0.1 all-reduce.5.cloned.1.call-start
  98.6 21.5 %all-gather.2.cloned.1.call-done = bf16[768,896]{0,1:T(8,128)(2,1)} async-done(((bf16[768,112]{0,1:T(8,128)(2,1)}), bf16[768,896]{0,1:T(8,128)(2,1)}) %all-gather.2.cloned.1.call-update) | async-done | bytes 1376272 | tf_op jit(solution)/shard_map/all_gather | solution.py:26
  120.1 1.7 fusion.9
  121.8 0.0 copy-done.10
  121.8 0.0 copy-start.3
  121.8 4.3 %fusion.26 = f32[768,608]{0,1:T(8,128)} fusion(bf16[896,608]{0,1:T(8,128)(2,1)} %param.21, bf16[768,896]{0,1:T(8,128)(2,1)} %all-gather.2.cloned.1.call-done, f32[896]{0:T(1024)S(1)} %copy-done.10, f32[768]{0:T(1024)S(1)} %add_rsqrt_fusion.1), kind=kOutput, calls=%fused_computation.37 | convolution fusion | flops 839516160 | bytes 4340224 | tf_op jit(solution)/shard_map/dot_general | solution.py:28
  126.1 0.0 copy-done
  126.1 0.0 copy-done.3
  126.1 6.0 %fusion.21 = f32[768,896]{0,1:T(8,128)} fusion(bf16[608,896]{1,0:T(8,128)(2,1)S(1)} %copy-done, f32[768,608]{0,1:T(8,128)} %fusion.26, bf16[896,608]{0,1:T(8,128)(2,1)} %param.22, bf16[768,896]{0,1:T(8,128)(2,1)S(1)} %copy-done.3, f32[896]{0:T(1024)S(1)} %copy-done.10, f32[768]{0:T(1024)S(1)} %add_rsqrt_fusion.1), kind=kOutput, calls=%fused_computation.34 | convolution fusion | flops 1679081472 | bytes 8182272 | tf_op jit(solution)/shard_map/dot_general | solution.py:31
  132.2 0.1 all-reduce.5.cloned.1.call-update
  132.2 57.4 %all-reduce.5.cloned.1.call-done = f32[768,896]{0,1:T(8,128)} async-done(((f32[768,896]{0,1:T(8,128)}), f32[768,896]{0,1:T(8,128)}) %all-reduce.5.cloned.1.call-update) | async-done | bytes 2752528 | tf_op jit(solution)/shard_map/psum | solution.py:32
  189.6 3.3 %fusion.6 = (f32[768]{0:T(1024)S(1)}, bf16[768,896]{0,1:T(8,128)(2,1)}) fusion(f32[768,896]{0,1:T(8,128)} %all-reduce.5.cloned.1.call-done, bf16[768,896]{0,1:T(8,128)(2,1)S(1)} %copy-done.3), kind=kLoop, calls=%fused_computation.18 | loop fusion | flops 4128000 | bytes 5508096 | tf_op jit(solution)/shard_map/reduce_sum | solution.py:11
  193.0 0.0 copy-start.5
  193.0 0.0 copy-start.11
  193.0 2.8 copy.15
  195.8 0.0 copy-done.5
  195.8 0.0 copy-done.11
  195.8 41.5 %fusion.33 = (f32[768]{0:T(1024)S(1)}, f32[768,18992]{0,1:T(8,128)}) fusion(bf16[896,18992]{0,1:T(8,128)(2,1)} %param.15, bf16[768,896]{0,1:T(8,128)(2,1)S(1)} %copy-done.5, f32[896]{0:T(1024)S(1)} %copy-done.11, f32[768]{0:T(1024)S(1)} %add_rsqrt_fusion), kind=kOutput, calls=%fused_computation.48 | convolution fusion | flops 26155192320 | bytes 93763072 | tf_op jit(solution)/shard_map/dot_general | solution.py:35
  237.3 14.4 %pmax.7 = f32[768]{0:T(1024)S(1)} all-reduce(f32[768]{0:T(1024)S(1)} %get-tuple-element.9), channel_id=1, replica_groups=mesh['dp'=2,'tp'=8] {'tp'}, use_global_device_ids=true, to_apply=%region_7.8 | all-reduce | flops 768 | bytes 6144 | tf_op jit(solution)/shard_map/pmax | solution.py:36
  251.8 18.6 %exponential_reduce_fusion = f32[768]{0:T(1024)S(1)} fusion(f32[768,18992]{0,1:T(8,128)} %get-tuple-element.10, f32[768]{0:T(1024)S(1)} %pmax.7), kind=kLoop, calls=%fused_computation.1 | loop fusion | flops 29170944 | bytes 58349568 | tf_op jit(solution)/shard_map/reduce_sum | solution.py:38
  270.4 13.7 %psum.23 = f32[768]{0:T(1024)S(1)} all-reduce(f32[768]{0:T(1024)S(1)} %exponential_reduce_fusion), channel_id=1, replica_groups=mesh['dp'=2,'tp'=8] {'tp'}, use_global_device_ids=true, to_apply=%region_9.10 | all-reduce | flops 768 | bytes 6144 | tf_op jit(solution)/shard_map/psum | solution.py:38
  284.1 0.0 copy-start.1
  284.1 39.4 %subtract_subtract_fusion = f32[768,18992]{0,1:T(8,128)} fusion(f32[768,18992]{0,1:T(8,128)} %get-tuple-element.10, f32[768]{0:T(1024)S(1)} %log.3, f32[768]{0:T(1024)S(1)} %pmax.7), kind=kLoop, calls=%fused_computation.2 | loop fusion | flops 29171712 | bytes 116692992 | tf_op jit(solution)/shard_map/sub | solution.py:39
  323.5 0.0 copy-done.1
  (6 shorter events, 0.0 us)
Async XLA Ops:
  7.2 119.0 %copy-start = (bf16[608,896]{1,0:T(8,128)(2,1)S(1)}, bf16[608,896]{1,0:T(8,128)(2,1)}, u32[]{:S(2)}) copy-start(bf16[608,896]{1,0:T(8,128)(2,1)} %param.23) | copy-start | bytes 3268612
  7.2 87.3 %all-reduce.3.cloned.1.call-start = ((), (), s32[]{:S(2)}) async-start(), calls=%async_computation | async-start | bytes 2752512 | tf_op jit(solution)/shard_map/psum | solution.py:23
  29.6 3.0 copy-start.2
  32.5 0.7 copy-start.7
  32.6 87.6 %all-gather.2.cloned.1.call-start = ((), (), s32[]{:S(2)}) async-start(), calls=%async_computation.1 | async-start | bytes 1548288 | tf_op jit(solution)/shard_map/all_gather | solution.py:26
  33.2 63.2 %copy-start.8 = (f32[896]{0:T(1024)S(1)}, f32[896]{0:T(1024)}, u32[]{:S(2)}) copy-start(f32[896]{0:T(1024)} %param.17) | copy-start | bytes 10756
  94.5 1.9 copy-start.4
  94.5 2.3 copy-start.6
  94.5 2.3 copy-start.9
  96.8 25.0 %copy-start.10 = (f32[896]{0:T(1024)S(1)}, f32[896]{0:T(1024)}, u32[]{:S(2)}) copy-start(f32[896]{0:T(1024)} %param.18) | copy-start | bytes 10756
  98.5 91.1 %all-reduce.5.cloned.1.call-start = ((), (), s32[]{:S(2)}) async-start(), calls=%async_computation.2 | async-start | bytes 5505024 | tf_op jit(solution)/shard_map/psum | solution.py:32
  121.8 4.3 %copy-start.3 = (bf16[768,896]{0,1:T(8,128)(2,1)S(1)}, bf16[768,896]{0,1:T(8,128)(2,1)}, u32[]{:S(2)}) copy-start(bf16[768,896]{0,1:T(8,128)(2,1)} %all-gather.2.cloned.1.call-done) | copy-start | bytes 4128772
  193.0 2.8 copy-start.5
  193.0 2.8 copy-start.11
  284.1 39.4 %copy-start.1 = (bf16[608,896]{1,0:T(8,128)(2,1)S(1)}, bf16[608,896]{1,0:T(8,128)(2,1)}, u32[]{:S(2)}) copy-start(bf16[608,896]{1,0:T(8,128)(2,1)} %param.23) | copy-start | bytes 3268612
Sparse Core Ops, SparseCore 0:
  32.7 61.7 all-reduce.2
  98.7 21.4 all-gather.1
  132.4 57.2 all-reduce.4
where the time goes:
time: 333 us; the launch traced here: 330 us
  waiting for transfers between devices  139 us (42%)
  other arithmetic  70.7 us (21%)
  matrix products  53.6 us (16%)
  blocking collectives  28.2 us (8%)
  local copies, waits for them, and re-layouts  24.6 us (7%)
  between operations  13.9 us (4%)
    psum x1, waiting for transfers between devices, draft_step(): emb_rows = lax.psum(picked, 'tp')  59.8 us
    psum x1, waiting for transfers between devices, draft_step(): down_sum = lax.psum(down_part, 'tp')  57.4 us
    dot_general x1, matrix products, draft_step(): logits = jnp.dot(out_norm, head_w, preferred_element_type=jnp.float32)  41.5 us
    sub x1, other arithmetic, draft_step(): return (new_u, shifted - jnp.log(row_sum)[:, None])  39.4 us
    gather x1, local copies, waits for them, and re-layouts, draft_step(): jnp.take(embedding, jnp.clip(local_ids, 0, vocab_local - 1), axis=0)  21.6 us
    all_gather x1, waiting for transfers between devices, draft_step(): proj_full = lax.all_gather(proj_cols, 'tp', axis=1, tiled=True)  21.5 us
    reduce_sum x1, other arithmetic, draft_step(): row_sum = lax.psum(jnp.sum(jnp.exp(shifted), axis=-1), 'tp')  18.6 us
    pmax x1, blocking collectives, draft_step(): row_max = lax.pmax(jnp.max(logits, axis=-1), 'tp')  14.4 us
  transfers between devices with their start and end apart: 3, of which 3 were waited for; matrix products, arithmetic and copies ran while one was open for 1% of the time, Pallas kernels for 0%

commit v1 on v0

v1 whole, which is shorter than its diff:
```python
import functools

import jax
import jax.numpy as jnp
from jax import lax
from jax.experimental import pallas as pl
from jax.experimental.pallas import tpu as pltpu
from jax.sharding import PartitionSpec as P

NORM_EPS = 1e-6
SLAB = 8
GROUP = 32
VOCAB_TILE = 528
F32 = jnp.float32
BF16 = jnp.bfloat16
MESH = pl.DeviceIdType.MESH


def gather_kernel(base_ref, want_ref, table_ref, out_ref, slabs, sems):
    groups = out_ref.shape[0] // GROUP
    span = GROUP * SLAB

    def issue(group, carry):
        for lane in range(GROUP):
            row = group * GROUP + lane
            base = pl.multiple_of(base_ref[row], SLAB)
            pltpu.make_async_copy(
                table_ref.at[pl.ds(base, SLAB), :],
                slabs.at[pl.ds(pl.multiple_of(row * SLAB, SLAB), SLAB), :],
                sems.at[group],
            ).start()
        return carry

    lax.fori_loop(0, groups, issue, 0)

    def select(group, carry):
        block = pl.ds(pl.multiple_of(group * span, span), span)
        rows = pl.ds(pl.multiple_of(group * GROUP, GROUP), GROUP)
        pltpu.make_async_copy(table_ref.at[pl.ds(0, span), :], slabs.at[block, :], sems.at[group]).wait()
        lanes = lax.broadcasted_iota(jnp.int32, (GROUP, span), 1)
        hot = jnp.where(want_ref[rows, :] == lanes, 1.0, 0.0).astype(BF16)
        out_ref[rows, :] = jnp.dot(hot, slabs[block, :], preferred_element_type=F32).astype(BF16)
        return carry

    lax.fori_loop(0, groups, select, 0)


def gather_rows(embedding, local_ids, owned):
    rows, dim = local_ids.shape[0], embedding.shape[1]
    spread = jnp.arange(rows, dtype=jnp.int32)
    ids = jnp.where(owned, local_ids, spread * SLAB % embedding.shape[0])
    place = spread % GROUP
    want = jnp.where(owned, place * SLAB + ids % SLAB, -1)[:, None]
    return pl.pallas_call(
        gather_kernel,
        out_shape=jax.ShapeDtypeStruct((rows, dim), BF16),
        in_specs=[
            pl.BlockSpec(memory_space=pltpu.SMEM),
            pl.BlockSpec(memory_space=pltpu.VMEM),
            pl.BlockSpec(memory_space=pl.ANY),
        ],
        out_specs=pl.BlockSpec(memory_space=pltpu.VMEM),
        scratch_shapes=[
            pltpu.VMEM((rows * SLAB, dim), BF16),
            pltpu.SemaphoreType.DMA((rows // GROUP,)),
        ],
        compiler_params=pltpu.CompilerParams(vmem_limit_bytes=24 << 20),
        name="gather_rows",
    )(ids // SLAB * SLAB, want, embedding)


def gain_row(gains, index):
    packed = gains[...]
    count = packed.shape[0] // 4
    return jnp.concatenate([packed[index * count + j : index * count + j + 1, :] for j in range(count)], axis=1)


def column_of(gain):
    return jnp.broadcast_to(gain, (128, gain.shape[1])).T


def norm_columns(src_ref, dst_ref, gain):
    gain = column_of(gain)
    dim, tokens = src_ref.shape
    for start in range(0, tokens, 128):
        lanes = pl.ds(start, 128)
        wide = src_ref[:, lanes].astype(F32)
        inv_rms = lax.rsqrt(jnp.sum(wide * wide, axis=0, keepdims=True) / dim + NORM_EPS)
        dst_ref[:, lanes] = (wide * inv_rms * gain).astype(dst_ref.dtype)


def norm_rows(wide, gain):
    inv_rms = lax.rsqrt(jnp.mean(wide * wide, axis=-1, keepdims=True) + NORM_EPS)
    return (wide * inv_rms * gain).astype(BF16)


def mix_kernel(
    n_tp,
    hidden_ref,
    picked_ref,
    gains,
    proj_t,
    gate_t,
    up_t,
    down,
    u_ref,
    o_ref,
    h_normed,
    e_full,
    p_full,
    n_full,
    a_full,
    u_full,
    comb_e,
    pair_e,
    far_e,
    part_d,
    pair_d,
    far_d,
    send_rs,
    recv_rs,
    send_ag,
    recv_ag,
):
    me = lax.axis_index("tp")
    chips = n_tp // 2
    chip, core = me // 2, me % 2
    partner = chip * 2 + 1 - core
    far = [lax.rem(chip + k, chips) for k in range(chips)]
    back = [lax.rem(chip + chips - k, chips) for k in range(chips)]
    tokens, dim = hidden_ref.shape
    t_rows = tokens // n_tp
    f_rows = proj_t.shape[0]

    barrier = pltpu.get_barrier_semaphore()
    for peer in [partner] + [far[k] * 2 + core for k in range(1, chips)]:
        pl.semaphore_signal(barrier, inc=1, device_id={"tp": peer}, device_id_type=MESH)
    pl.semaphore_wait(barrier, chips)

    def push(src, dst, send_sem, recv_sem, device):
        copy = pltpu.make_async_remote_copy(
            src_ref=src, dst_ref=dst, send_sem=send_sem, recv_sem=recv_sem, device_id={"tp": device}, device_id_type=MESH
        )
        copy.start()
        return copy

    def rows_of(device, size):
        return pl.ds(pl.multiple_of(device * size, 16), size)

    def pair_send(src, size, landing, stage):
        return [
            push(
                src.at[rows_of(c * 2 + 1 - core, size), :],
                landing.at[c],
                send_rs.at[stage, c],
                recv_rs.at[stage, c],
                partner,
            )
            for c in range(chips)
        ]

    def far_send(src, landing, k, stage):
        return push(src, landing.at[k - 1], send_rs.at[stage, k], recv_rs.at[stage, k], far[k] * 2 + core)

    def all_gather(full, size, stage):
        own = full.at[rows_of(me, size), :]
        sends = {}
        for k in [2, 1, 3]:
            sends[k] = push(own, own, send_ag.at[stage, k], recv_ag.at[stage, k], far[k] * 2 + core)
        near = push(own, own, send_ag.at[stage, 0], recv_ag.at[stage, 0], partner)
        passed = []
        for k in [1, 3, 2]:
            sends[k].wait_recv()
            block = full.at[rows_of(back[k] * 2 + core, size), :]
            passed.append(push(block, block, send_ag.at[stage, chips + k], recv_ag.at[stage, chips + k], partner))
        near.wait_recv()
        for copy in passed:
            copy.wait_recv()
        for copy in [near] + passed + list(sends.values()):
            copy.wait_send()

    e_pair = pair_send(picked_ref, t_rows, pair_e, 0)

    def norm_hidden(step, carry):
        rows = pl.ds(pl.multiple_of(step * t_rows, 16), t_rows)
        h_normed[rows, :] = norm_rows(hidden_ref[rows, :].astype(F32), gain_row(gains, 0))
        return carry

    e_far = {}
    for k in [2, 1, 3, 0]:
        c = far[k]
        for copy in [e_pair] if k == 2 else []:
            for one in copy:
                one.wait()
        comb_e[k] = picked_ref[rows_of(c * 2 + core, t_rows), :] + pair_e[c]
        if k:
            e_far[k] = far_send(comb_e.at[k], far_e, k, 1)
    lax.fori_loop(0, n_tp, norm_hidden, 0)
    total = comb_e[0]
    for k in [1, 3, 2]:
        e_far[k].wait()
        total = total + far_e[k - 1]
    e_full[rows_of(me, t_rows), :] = norm_rows(total.astype(F32), gain_row(gains, 1))
    all_gather(e_full, t_rows, 0)

    contract_last = (((1,), (1,)), ((), ()))
    p_own = lax.dot_general(proj_t[:, :dim], h_normed[...], contract_last, preferred_element_type=F32)
    p_own = p_own + lax.dot_general(proj_t[:, dim:], e_full[...], contract_last, preferred_element_type=F32)
    p_full[rows_of(me, f_rows), :] = p_own.astype(BF16)
    all_gather(p_full, f_rows, 1)

    norm_columns(p_full, n_full, gain_row(gains, 2))
    for start in range(0, tokens, 256):
        lanes = pl.ds(start, 256)
        gate_val = jnp.dot(gate_t[...], n_full[:, lanes], preferred_element_type=F32)
        up_val = jnp.dot(up_t[...], n_full[:, lanes], preferred_element_type=F32)
        a_full[:, lanes] = (gate_val * jax.nn.sigmoid(gate_val) * up_val).astype(BF16)
    contract_first = (((0,), (0,)), ((), ()))
    for start in range(0, tokens, 256):
        lanes = pl.ds(start, 256)
        part_d[:, lanes] = lax.dot_general(down[...], a_full[:, lanes], contract_first, preferred_element_type=F32)

    d_pair = pair_send(part_d, f_rows, pair_d, 2)
    d_far = {}
    for one in d_pair:
        one.wait()
    for k in [2, 1, 3, 0]:
        c = far[k]
        pair_d[c] = part_d[rows_of(c * 2 + core, f_rows), :] + pair_d[c]
        if k:
            d_far[k] = far_send(pair_d.at[c], far_d, k, 3)
    summed = pair_d[chip]
    for k in [1, 3, 2]:
        d_far[k].wait()
        summed = summed + far_d[k - 1]
    own = rows_of(me, f_rows)
    u_full[own, :] = (p_full[own, :].astype(F32) + summed).astype(BF16)
    all_gather(u_full, f_rows, 2)

    norm_columns(u_full, o_ref, gain_row(gains, 3))
    for start in range(0, tokens, 128):
        u_ref[pl.ds(start, 128), :] = u_full[:, pl.ds(start, 128)].T


def mix(n_tp, hidden, picked, gains, proj_w, w_gate, w_up, w_down):
    tokens, dim = hidden.shape
    chips = n_tp // 2
    t_rows, f_rows, ffn = tokens // n_tp, proj_w.shape[1], w_gate.shape[1]
    vmem = pl.BlockSpec(memory_space=pltpu.VMEM)
    return pl.pallas_call(
        functools.partial(mix_kernel, n_tp),
        out_shape=(jax.ShapeDtypeStruct((tokens, dim), BF16), jax.ShapeDtypeStruct((dim, tokens), BF16)),
        in_specs=[vmem] * 7,
        out_specs=(vmem, vmem),
        scratch_shapes=[
            pltpu.VMEM((tokens, dim), BF16),
            pltpu.VMEM((tokens, dim), BF16),
            pltpu.VMEM((dim, tokens), BF16),
            pltpu.VMEM((dim, tokens), BF16),
            pltpu.VMEM((ffn, tokens), BF16),
            pltpu.VMEM((dim, tokens), BF16),
            pltpu.VMEM((chips, t_rows, dim), BF16),
            pltpu.VMEM((chips, t_rows, dim), BF16),
            pltpu.VMEM((chips - 1, t_rows, dim), BF16),
            pltpu.VMEM((dim, tokens), F32),
            pltpu.VMEM((chips, f_rows, tokens), F32),
            pltpu.VMEM((chips - 1, f_rows, tokens), F32),
            pltpu.SemaphoreType.DMA((4, chips)),
            pltpu.SemaphoreType.DMA((4, chips)),
            pltpu.SemaphoreType.DMA((3, 2 * chips)),
            pltpu.SemaphoreType.DMA((3, 2 * chips)),
        ],
        compiler_params=pltpu.CompilerParams(collective_id=0, has_side_effects=True, vmem_limit_bytes=48 << 20),
        name="mix",
    )(
        hidden,
        picked,
        gains,
        proj_w.T,
        w_gate.T,
        w_up.T,
        w_down,
    )


def stats_kernel(vocab, head_ref, o_ref, max_ref, sum_ref, logits):
    step = pl.program_id(0)
    rows, tokens = logits.shape

    @pl.when(step == 0)
    def _():
        max_ref[...] = jnp.full_like(max_ref, -jnp.inf)
        sum_ref[...] = jnp.zeros_like(sum_ref)

    left = vocab - step * rows
    for start in range(0, tokens, 256):
        lanes = pl.ds(start, 256)
        z = jnp.dot(head_ref[...], o_ref[:, lanes], preferred_element_type=F32)
        index = lax.broadcasted_iota(jnp.int32, z.shape, 0)
        z = jnp.where(index < left, z, -jnp.inf).reshape(rows // 8, 8, 256)
        old = max_ref[:, lanes]
        new = jnp.maximum(old, jnp.max(z, axis=0))
        sum_ref[:, lanes] = sum_ref[:, lanes] * jnp.exp(old - new) + jnp.sum(jnp.exp(z - new[None]), axis=0)
        max_ref[:, lanes] = new


def head_stats(head_t, o_t):
    vocab, dim = head_t.shape
    tokens = o_t.shape[1]
    keep = pl.BlockSpec((8, tokens), lambda i: (0, 0))
    return pl.pallas_call(
        functools.partial(stats_kernel, vocab),
        out_shape=(jax.ShapeDtypeStruct((8, tokens), F32), jax.ShapeDtypeStruct((8, tokens), F32)),
        grid=(pl.cdiv(vocab, VOCAB_TILE),),
        in_specs=[
            pl.BlockSpec((VOCAB_TILE, dim), lambda i: (i, 0)),
            pl.BlockSpec((dim, tokens), lambda i: (0, 0)),
        ],
        out_specs=(keep, keep),
        scratch_shapes=[pltpu.VMEM((VOCAB_TILE, tokens), F32)],
        compiler_params=pltpu.CompilerParams(dimension_semantics=("arbitrary",), vmem_limit_bytes=32 << 20),
        name="head_stats",
    )(head_t, o_t)


def merge_kernel(n_tp, max_ref, sum_ref, lse_ref, mine, theirs, send_sem, recv_sem):
    me = lax.axis_index("tp")
    barrier = pltpu.get_barrier_semaphore()
    for k in range(1, n_tp):
        peer = lax.rem(me + k, n_tp)
        pl.semaphore_signal(barrier, inc=1, device_id={"tp": peer}, device_id_type=MESH)
    tokens = max_ref.shape[1]
    top = jnp.max(max_ref[...], axis=0, keepdims=True)
    scaled = jnp.sum(sum_ref[...] * jnp.exp(max_ref[...] - top), axis=0, keepdims=True)
    mine[...] = jnp.concatenate([jnp.broadcast_to(top, (8, tokens)), jnp.broadcast_to(scaled, (8, tokens))], axis=0)
    pl.semaphore_wait(barrier, n_tp - 1)
    copies = []
    for k in range(1, n_tp):
        copy = pltpu.make_async_remote_copy(
            src_ref=mine,
            dst_ref=theirs.at[k - 1],
            send_sem=send_sem.at[k - 1],
            recv_sem=recv_sem.at[k - 1],
            device_id={"tp": lax.rem(me + k, n_tp)},
            device_id_type=MESH,
        )
        copy.start()
        copies.append(copy)
    for copy in copies:
        copy.wait()
    best, total = mine[:8, :], mine[8:, :]
    for k in range(n_tp - 1):
        other, extra = theirs[k, :8, :], theirs[k, 8:, :]
        new = jnp.maximum(best, other)
        total = total * jnp.exp(best - new) + extra * jnp.exp(other - new)
        best = new
    lse_ref[...] = best + jnp.log(total)


def merge(n_tp, maxima, sums):
    tokens = maxima.shape[1]
    vmem = pl.BlockSpec(memory_space=pltpu.VMEM)
    return pl.pallas_call(
        functools.partial(merge_kernel, n_tp),
        out_shape=jax.ShapeDtypeStruct((8, tokens), F32),
        in_specs=[vmem, vmem],
        out_specs=vmem,
        scratch_shapes=[
            pltpu.VMEM((16, tokens), F32),
            pltpu.VMEM((n_tp - 1, 16, tokens), F32),
            pltpu.SemaphoreType.DMA((n_tp - 1,)),
            pltpu.SemaphoreType.DMA((n_tp - 1,)),
        ],
        compiler_params=pltpu.CompilerParams(collective_id=1, has_side_effects=True),
        name="merge",
    )(maxima, sums)


def logp_kernel(head_ref, o_ref, lse_ref, out_ref):
    tokens = o_ref.shape[1]
    for start in range(0, tokens, 256):
        lanes = pl.ds(start, 256)
        z = jnp.dot(head_ref[...], o_ref[:, lanes], preferred_element_type=F32)
        out_ref[:, lanes] = z - lse_ref[0:1, lanes]


def head_logp(head_t, o_t, lse):
    vocab, dim = head_t.shape
    tokens = o_t.shape[1]
    return pl.pallas_call(
        logp_kernel,
        out_shape=jax.ShapeDtypeStruct((vocab, tokens), F32),
        grid=(pl.cdiv(vocab, VOCAB_TILE),),
        in_specs=[
            pl.BlockSpec((VOCAB_TILE, dim), lambda i: (i, 0)),
            pl.BlockSpec((dim, tokens), lambda i: (0, 0)),
            pl.BlockSpec((8, tokens), lambda i: (0, 0)),
        ],
        out_specs=pl.BlockSpec((VOCAB_TILE, tokens), lambda i: (i, 0)),
        compiler_params=pltpu.CompilerParams(dimension_semantics=("arbitrary",), vmem_limit_bytes=32 << 20),
        name="head_logp",
    )(head_t, o_t, lse)


def solution(mesh):
    n_tp = mesh.shape["tp"]

    def draft_step(hidden, tokens, embedding, head_w, h_norm, e_norm, f_norm, o_norm, proj_w, w_gate, w_up, w_down):
        vocab_local = embedding.shape[0]
        local_ids = tokens - lax.axis_index("tp") * vocab_local
        owned = (local_ids >= 0) & (local_ids < vocab_local)
        picked = gather_rows(embedding, local_ids, owned)
        gains = jnp.concatenate([h_norm, e_norm, f_norm, o_norm]).reshape(-1, 128)
        new_u, out_t = mix(n_tp, hidden, picked, gains, proj_w, w_gate, w_up, w_down)
        head_t = head_w.T
        lse = merge(n_tp, *head_stats(head_t, out_t))
        return new_u, head_logp(head_t, out_t, lse).T

    specs_in = (
        P("dp", None), P("dp"), P("tp", None), P(None, "tp"), P(None), P(None), P(None), P(None),
        P(None, "tp"), P(None, "tp"), P(None, "tp"), P("tp", None),
    )
    specs_out = (P("dp", None), P("dp", "tp"))
    return jax.shard_map(draft_step, mesh=mesh, in_specs=specs_in, out_specs=specs_out, check_vma=False)
```

time: 333 us -> 208 us (0.62)
  Pallas kernels: 0 us -> 198 us
  waiting for transfers between devices: 139 us -> 0 us
  other arithmetic: 70.7 us -> 1.46 us
  matrix products: 53.6 us -> 0 us
  blocking collectives: 28.2 us -> 0 us
  local copies, waits for them, and re-layouts: 24.6 us -> 5.61 us
  between operations: 13.9 us -> 0.75 us
    pallas_call x0 -> x5, Pallas kernels: none -> 198 us  [the longest x1 79.1 us: mix(): pl.pallas_call(functools.partial(mix_kernel, n_tp), out_shape=(jax.ShapeD...]
    psum x2 -> x0, waiting for transfers between devices: 117 us -> none  [the longest x1 59.8 us: draft_step(): emb_rows = lax.psum(picked, 'tp')]
    dot_general x4 -> x0, matrix products: 53.6 us -> none  [the longest x1 41.5 us: draft_step(): logits = jnp.dot(out_norm, head_w, preferred_element_type=jnp.float32)]
    sub x1 -> x0, other arithmetic: 39.4 us -> none  [draft_step(): return (new_u, shifted - jnp.log(row_sum)[:, None])]
    reduce_sum x5 -> x0, other arithmetic: 25.8 us -> none  [the longest x1 18.6 us: draft_step(): row_sum = lax.psum(jnp.sum(jnp.exp(shifted), axis=-1), 'tp')]
    gather x1 -> x0, local copies, waits for them, and re-layouts: 21.6 us -> none  [draft_step(): jnp.take(embedding, jnp.clip(local_ids, 0, vocab_local - 1), axis=0)]
    all_gather x1 -> x0, waiting for transfers between devices: 21.5 us -> none  [draft_step(): proj_full = lax.all_gather(proj_cols, 'tp', axis=1, tiled=True)]
    pmax x1 -> x0, blocking collectives: 14.4 us -> none  [draft_step(): row_max = lax.pmax(jnp.max(logits, axis=-1), 'tp')]
  transfers between devices with their start and end apart: 3 -> 0, of which waited for: 3 -> 0; matrix products, arithmetic and copies ran while one was open for 1% -> 0% of each run, Pallas kernels for 0% -> 0%
where the time goes in v1:
time: 208 us; the launch traced here: 206 us
  Pallas kernels  198 us (95%)
  local copies, waits for them, and re-layouts  5.61 us (3%)
    pallas_call x1, Pallas kernels, mix(): pl.pallas_call(functools.partial(mix_kernel, n_tp), out_shape=(jax.ShapeD...  79.1 us
    pallas_call x1, Pallas kernels, head_logp(): pl.pallas_call(logp_kernel, out_shape=jax.ShapeDtypeStruct((vocab, tokens...  53.2 us
    pallas_call x1, Pallas kernels, head_stats(): pl.pallas_call(functools.partial(stats_kernel, vocab), out_shape=(jax.Sha...  46.5 us
    pallas_call x1, Pallas kernels, merge(): pl.pallas_call(functools.partial(merge_kernel, n_tp), out_shape=jax.Shape...  9.95 us
    pallas_call x1, Pallas kernels, gather_rows(): pl.pallas_call(gather_kernel, out_shape=jax.ShapeDtypeStruct((rows, dim),...  9.04 us
    unnamed x21, local copies, waits for them, and re-layouts  5.45 us

profile of v1, /device:TPU:113, one launch (start us, length us, event | category | flops | bytes accessed | tf_op | source)
XLA Modules:
  0.0 205.6 jit_solution(12885066246068960087)
XLA Ops:
  0.6 0.7 fusion.4
  1.3 0.7 pad_maximum_fusion.gains
  2.1 0.2 broadcast_in_dim.6.want_ref
  2.3 0.0 copy-start.3
  2.3 0.0 copy-start.4
  2.3 0.0 copy-start.5
  2.3 0.0 copy-start.6
  2.3 9.0 %gather_rows.1.picked_ref = bf16[768,896]{1,0:T(8,128)(2,1)S(1)} custom-call(s32[768]{0:T(1024)S(1)} %get-tuple-element.11.base_ref, s32[768,1]{1,0:T(8,128)S(1)} %broadcast_in_dim.6.want_ref, bf16[18992,896]{1,0:T(8,128)(2,1)} %table_ref.1), custom_call_target="tpu_custom_call" | custom-call | tf_op jit(solution)/shard_map/gather_rows/pallas_call | solution.py:54
  11.4 0.0 copy-start.2
  11.4 1.1 copy-done.2
  12.4 0.0 copy-done.3
  12.4 0.0 copy-done.4
  12.4 0.0 copy-done.5
  12.4 0.0 copy-done.6
  12.4 79.1 %mix.1 = (bf16[768,896]{1,0:T(8,128)(2,1)S(1)}, bf16[896,768]{1,0:T(8,128)(2,1)}) custom-call(bf16[768,896]{1,0:T(8,128)(2,1)} %hidden_ref.1, bf16[768,896]{1,0:T(8,128)(2,1)} %copy-done.2, f32[28,128]{1,0:T(8,128)S(1)} %pad_maximum_fusion.gains, bf16[112,1792]{1,0:T(8,128)(2,1)S(1)} %bitcast.11, bf16[608,896]{1,0:T(8,128)(2,1)S(1)} %bitcast.9, ...), custom_call_target="tpu_custom_call" | custom-call | tf_op jit(solution)/shard_map/mix/pallas_call | solution.py:250
  91.6 0.0 copy-start
  91.6 1.3 copy-done
  92.9 0.0 copy-start.1
  92.9 46.5 %head_stats.1 = (f32[8,768]{1,0:T(8,128)S(1)}, f32[8,768]{1,0:T(8,128)S(1)}) custom-call(bf16[18992,896]{1,0:T(8,128)(2,1)} %bitcast.12, bf16[896,768]{1,0:T(8,128)(2,1)S(1)} %copy-done), custom_call_target="tpu_custom_call" | custom-call | tf_op jit(solution)/shard_map/head_stats/pallas_call | solution.py:311
  139.4 0.0 copy-start.8
  139.4 0.6 copy-done.8
  140.0 0.0 copy-start.9
  140.0 0.6 copy-done.9
  140.6 9.9 %merge.1.lse_ref = f32[8,768]{1,0:T(8,128)} custom-call(f32[8,768]{1,0:T(8,128)} %copy-done.8, f32[8,768]{1,0:T(8,128)} %copy-done.9), custom_call_target="tpu_custom_call" | custom-call | tf_op jit(solution)/shard_map/merge/pallas_call | solution.py:363
  150.6 0.0 copy-done.1
  150.6 0.0 copy-start.7
  150.6 0.7 copy-done.7
  151.3 53.2 %head_logp.1 = f32[18992,768]{1,0:T(8,128)} custom-call(bf16[18992,896]{1,0:T(8,128)(2,1)} %bitcast.13, bf16[896,768]{1,0:T(8,128)(2,1)S(1)} %copy-done.1, f32[8,768]{1,0:T(8,128)S(1)} %copy-done.7), custom_call_target="tpu_custom_call" | custom-call | tf_op jit(solution)/shard_map/head_logp/pallas_call | solution.py:390
  204.5 1.1 copy.16
Async XLA Ops:
  2.3 10.2 %copy-start.3 = (bf16[896,608]{0,1:T(8,128)(2,1)S(1)}, bf16[896,608]{0,1:T(8,128)(2,1)}, u32[]{:S(2)}) copy-start(bf16[896,608]{0,1:T(8,128)(2,1)} %param.21) | copy-start | bytes 3268612
  2.3 10.2 %copy-start.4 = (bf16[896,608]{0,1:T(8,128)(2,1)S(1)}, bf16[896,608]{0,1:T(8,128)(2,1)}, u32[]{:S(2)}) copy-start(bf16[896,608]{0,1:T(8,128)(2,1)} %param.22) | copy-start | bytes 3268612
  2.3 10.2 %copy-start.5 = (bf16[608,896]{1,0:T(8,128)(2,1)S(1)}, bf16[608,896]{1,0:T(8,128)(2,1)}, u32[]{:S(2)}) copy-start(bf16[608,896]{1,0:T(8,128)(2,1)} %down.1) | copy-start | bytes 3268612
  2.3 10.2 %copy-start.6 = (bf16[1792,112]{0,1:T(8,128)(2,1)S(1)}, bf16[1792,112]{0,1:T(8,128)(2,1)}, u32[]{:S(2)}) copy-start(bf16[1792,112]{0,1:T(8,128)(2,1)} %param.20) | copy-start | bytes 1204228
  11.4 1.1 copy-start.2
  91.6 1.3 copy-start
  92.9 57.6 %copy-start.1 = (bf16[896,768]{1,0:T(8,128)(2,1)S(1)}, bf16[896,768]{1,0:T(8,128)(2,1)}, u32[]{:S(2)}) copy-start(bf16[896,768]{1,0:T(8,128)(2,1)} %get-tuple-element.7.o_ref) | copy-start | bytes 4128772
  139.4 0.6 copy-start.8
  140.0 0.6 copy-start.9
  150.6 0.7 copy-start.7

commit v2 on v1

v2 whole, which is shorter than its diff:
```python
import functools

import jax
import jax.numpy as jnp
from jax import lax
from jax.experimental import pallas as pl
from jax.experimental.pallas import tpu as pltpu
from jax.sharding import PartitionSpec as P

NORM_EPS = 1e-6
SLAB = 8
GROUP = 32
TILE = 1056
HALF = TILE // 2
LANES = 256
KEEPS = 6
KEEP_TILES = 12
CHUNK = 256
LOWEST = float(jnp.finfo(jnp.float32).min)
F32 = jnp.float32
BF16 = jnp.bfloat16
MESH = pl.DeviceIdType.MESH


def gather_kernel(base_ref, want_ref, table_ref, out_ref, slabs, sems):
    groups = out_ref.shape[0] // GROUP
    span = GROUP * SLAB

    def issue(group, carry):
        for lane in range(GROUP):
            row = group * GROUP + lane
            base = pl.multiple_of(base_ref[row], SLAB)
            pltpu.make_async_copy(
                table_ref.at[pl.ds(base, SLAB), :],
                slabs.at[pl.ds(pl.multiple_of(row * SLAB, SLAB), SLAB), :],
                sems.at[group],
            ).start()
        return carry

    lax.fori_loop(0, groups, issue, 0)

    def select(group, carry):
        block = pl.ds(pl.multiple_of(group * span, span), span)
        rows = pl.ds(pl.multiple_of(group * GROUP, GROUP), GROUP)
        pltpu.make_async_copy(table_ref.at[pl.ds(0, span), :], slabs.at[block, :], sems.at[group]).wait()
        lanes = lax.broadcasted_iota(jnp.int32, (GROUP, span), 1)
        hot = jnp.where(want_ref[rows, :] == lanes, 1.0, 0.0).astype(BF16)
        out_ref[rows, :] = jnp.dot(hot, slabs[block, :], preferred_element_type=F32).astype(BF16)
        return carry

    lax.fori_loop(0, groups, select, 0)


def gather_rows(embedding, local_ids, owned):
    rows, dim = local_ids.shape[0], embedding.shape[1]
    spread = jnp.arange(rows, dtype=jnp.int32)
    ids = jnp.where(owned, local_ids, spread * SLAB % embedding.shape[0])
    place = spread % GROUP
    want = jnp.where(owned, place * SLAB + ids % SLAB, -1)[:, None]
    return pl.pallas_call(
        gather_kernel,
        out_shape=jax.ShapeDtypeStruct((rows, dim), BF16),
        in_specs=[
            pl.BlockSpec(memory_space=pltpu.SMEM),
            pl.BlockSpec(memory_space=pltpu.VMEM),
            pl.BlockSpec(memory_space=pl.ANY),
        ],
        out_specs=pl.BlockSpec(memory_space=pltpu.VMEM),
        scratch_shapes=[
            pltpu.VMEM((rows * SLAB, dim), BF16),
            pltpu.SemaphoreType.DMA((rows // GROUP,)),
        ],
        compiler_params=pltpu.CompilerParams(vmem_limit_bytes=24 << 20),
        name="gather_rows",
    )(ids // SLAB * SLAB, want, embedding)


def gain_row(gains, index):
    packed = gains[...]
    count = packed.shape[0] // 4
    return jnp.concatenate([packed[index * count + j : index * count + j + 1, :] for j in range(count)], axis=1)


def column_of(gain):
    return jnp.broadcast_to(gain, (128, gain.shape[1])).T


def norm_columns(src_ref, dst_ref, gain):
    gain = column_of(gain)
    dim, tokens = src_ref.shape
    for start in range(0, tokens, 128):
        lanes = pl.ds(start, 128)
        wide = src_ref[:, lanes].astype(F32)
        inv_rms = lax.rsqrt(jnp.sum(wide * wide, axis=0, keepdims=True) / dim + NORM_EPS)
        dst_ref[:, lanes] = (wide * inv_rms * gain).astype(dst_ref.dtype)


def norm_rows(wide, gain):
    inv_rms = lax.rsqrt(jnp.mean(wide * wide, axis=-1, keepdims=True) + NORM_EPS)
    return (wide * inv_rms * gain).astype(BF16)


def mix_kernel(
    n_tp,
    hidden_ref,
    picked_ref,
    gains,
    proj_t,
    gate_t,
    up_t,
    down,
    u_ref,
    o_ref,
    h_normed,
    e_full,
    p_full,
    n_full,
    a_full,
    u_full,
    comb_e,
    pair_e,
    far_e,
    part_d,
    pair_d,
    far_d,
    send_rs,
    recv_rs,
    send_ag,
    recv_ag,
):
    me = lax.axis_index("tp")
    chips = n_tp // 2
    chip, core = me // 2, me % 2
    partner = chip * 2 + 1 - core
    far = [lax.rem(chip + k, chips) for k in range(chips)]
    back = [lax.rem(chip + chips - k, chips) for k in range(chips)]
    tokens, dim = hidden_ref.shape
    chunks = tokens // CHUNK
    t_rows = CHUNK // n_tp
    f_rows = proj_t.shape[0]
    order = [2, 1, 3]
    contract_last = (((1,), (1,)), ((), ()))
    contract_first = (((0,), (0,)), ((), ()))

    barrier = pltpu.get_barrier_semaphore()
    for peer in [partner] + [far[k] * 2 + core for k in range(1, chips)]:
        pl.semaphore_signal(barrier, inc=1, device_id={"tp": peer}, device_id_type=MESH)
    pl.semaphore_wait(barrier, chips)

    def push(src, dst, send_sem, recv_sem, device):
        copy = pltpu.make_async_remote_copy(
            src_ref=src, dst_ref=dst, send_sem=send_sem, recv_sem=recv_sem, device_id={"tp": device}, device_id_type=MESH
        )
        copy.start()
        return copy

    def token_block(chunk):
        return lambda device: (pl.ds(pl.multiple_of(chunk * CHUNK + device * t_rows, 16), t_rows), slice(None))

    def feature_block(chunk):
        return lambda device: (pl.ds(pl.multiple_of(device * f_rows, 16), f_rows), pl.ds(chunk * CHUNK, CHUNK))

    def pair_send(src, block, landing, stage, chunk):
        return [
            push(
                src.at[block(c * 2 + 1 - core)],
                landing.at[chunk, c],
                send_rs.at[stage, chunk, c],
                recv_rs.at[stage, chunk, c],
                partner,
            )
            for c in range(chips)
        ]

    def far_send(src, landing, k, stage, chunk):
        return push(
            src, landing.at[chunk, k - 1], send_rs.at[stage, chunk, k], recv_rs.at[stage, chunk, k], far[k] * 2 + core
        )

    def gather_start(full, block, stage, chunk):
        own = full.at[block(me)]
        sends = {
            k: push(own, own, send_ag.at[stage, chunk, k], recv_ag.at[stage, chunk, k], far[k] * 2 + core) for k in order
        }
        near = push(own, own, send_ag.at[stage, chunk, 0], recv_ag.at[stage, chunk, 0], partner)
        return sends, near

    def gather_pass(state, full, block, stage, chunk):
        sends, near = state
        passed = []
        for k in [1, 3, 2]:
            sends[k].wait_recv()
            view = full.at[block(back[k] * 2 + core)]
            passed.append(
                push(view, view, send_ag.at[stage, chunk, chips + k], recv_ag.at[stage, chunk, chips + k], partner)
            )
        return [near] + passed, list(sends.values())

    def gather_end(state):
        local, sends = state
        for copy in local:
            copy.wait()
        for copy in sends:
            copy.wait_send()

    live = [None] * chunks

    def e_start(chunk):
        live[chunk] = pair_send(picked_ref, token_block(chunk), pair_e, 0, chunk)

    def h_norm(chunk):
        for start in range(0, CHUNK, 64):
            rows = pl.ds(chunk * CHUNK + start, 64)
            h_normed[rows, :] = norm_rows(hidden_ref[rows, :].astype(F32), gain_row(gains, 0))

    def e_mid(chunk):
        for copy in live[chunk]:
            copy.wait()
        block, sends = token_block(chunk), {}
        for k in order + [0]:
            comb_e[chunk, k] = picked_ref[block(far[k] * 2 + core)] + pair_e[chunk, far[k]]
            if k:
                sends[k] = far_send(comb_e.at[chunk, k], far_e, k, 1, chunk)
        live[chunk] = sends

    def e_end(chunk):
        total = comb_e[chunk, 0]
        for k in [1, 3, 2]:
            live[chunk][k].wait()
            total = total + far_e[chunk, k - 1]
        block = token_block(chunk)
        e_full[block(me)] = norm_rows(total.astype(F32), gain_row(gains, 1))
        live[chunk] = gather_start(e_full, block, 0, chunk)

    def e_pass(chunk):
        live[chunk] = gather_pass(live[chunk], e_full, token_block(chunk), 0, chunk)

    def project(chunk):
        gather_end(live[chunk])
        rows, block = pl.ds(chunk * CHUNK, CHUNK), feature_block(chunk)
        p_own = lax.dot_general(proj_t[:, :dim], h_normed[rows, :], contract_last, preferred_element_type=F32)
        p_own = p_own + lax.dot_general(proj_t[:, dim:], e_full[rows, :], contract_last, preferred_element_type=F32)
        p_full[block(me)] = p_own.astype(BF16)
        live[chunk] = gather_start(p_full, block, 1, chunk)

    def p_pass(chunk):
        live[chunk] = gather_pass(live[chunk], p_full, feature_block(chunk), 1, chunk)

    def feed_forward(chunk):
        gather_end(live[chunk])
        lanes = pl.ds(chunk * CHUNK, CHUNK)
        norm_columns(p_full.at[:, lanes], n_full.at[:, lanes], gain_row(gains, 2))
        gate_val = jnp.dot(gate_t[...], n_full[:, lanes], preferred_element_type=F32)
        up_val = jnp.dot(up_t[...], n_full[:, lanes], preferred_element_type=F32)
        a_full[:, lanes] = (gate_val * jax.nn.sigmoid(gate_val) * up_val).astype(BF16)
        part_d[:, lanes] = lax.dot_general(down[...], a_full[:, lanes], contract_first, preferred_element_type=F32)
        live[chunk] = pair_send(part_d, feature_block(chunk), pair_d, 2, chunk)

    def d_mid(chunk):
        for copy in live[chunk]:
            copy.wait()
        block, sends = feature_block(chunk), {}
        for k in order + [0]:
            pair_d[chunk, far[k]] = part_d[block(far[k] * 2 + core)] + pair_d[chunk, far[k]]
            if k:
                sends[k] = far_send(pair_d.at[chunk, far[k]], far_d, k, 3, chunk)
        live[chunk] = sends

    def d_end(chunk):
        summed = pair_d[chunk, chip]
        for k in [1, 3, 2]:
            live[chunk][k].wait()
            summed = summed + far_d[chunk, k - 1]
        block = feature_block(chunk)
        u_full[block(me)] = (p_full[block(me)].astype(F32) + summed).astype(BF16)
        live[chunk] = gather_start(u_full, block, 2, chunk)

    def u_pass(chunk):
        live[chunk] = gather_pass(live[chunk], u_full, feature_block(chunk), 2, chunk)

    def finish(chunk):
        gather_end(live[chunk])
        lanes = pl.ds(chunk * CHUNK, CHUNK)
        norm_columns(u_full.at[:, lanes], o_ref.at[:, lanes], gain_row(gains, 3))
        for start in range(chunk * CHUNK, (chunk + 1) * CHUNK, 128):
            u_ref[pl.ds(start, 128), :] = u_full[:, pl.ds(start, 128)].T

    for stage in (e_start, e_mid, h_norm, e_end, e_pass, project, p_pass, feed_forward, d_mid, d_end, u_pass, finish):
        for chunk in range(chunks):
            stage(chunk)


def mix(n_tp, hidden, picked, gains, proj_w, w_gate, w_up, w_down):
    tokens, dim = hidden.shape
    chips, chunks = n_tp // 2, tokens // CHUNK
    t_rows, f_rows, ffn = CHUNK // n_tp, proj_w.shape[1], w_gate.shape[1]
    vmem = pl.BlockSpec(memory_space=pltpu.VMEM)
    return pl.pallas_call(
        functools.partial(mix_kernel, n_tp),
        out_shape=(jax.ShapeDtypeStruct((tokens, dim), BF16), jax.ShapeDtypeStruct((dim, tokens), BF16)),
        in_specs=[vmem] * 7,
        out_specs=(vmem, vmem),
        scratch_shapes=[
            pltpu.VMEM((tokens, dim), BF16),
            pltpu.VMEM((tokens, dim), BF16),
            pltpu.VMEM((dim, tokens), BF16),
            pltpu.VMEM((dim, tokens), BF16),
            pltpu.VMEM((ffn, tokens), BF16),
            pltpu.VMEM((dim, tokens), BF16),
            pltpu.VMEM((chunks, chips, t_rows, dim), BF16),
            pltpu.VMEM((chunks, chips, t_rows, dim), BF16),
            pltpu.VMEM((chunks, chips - 1, t_rows, dim), BF16),
            pltpu.VMEM((dim, tokens), F32),
            pltpu.VMEM((chunks, chips, f_rows, CHUNK), F32),
            pltpu.VMEM((chunks, chips - 1, f_rows, CHUNK), F32),
            pltpu.SemaphoreType.DMA((4, chunks, chips)),
            pltpu.SemaphoreType.DMA((4, chunks, chips)),
            pltpu.SemaphoreType.DMA((3, chunks, 2 * chips)),
            pltpu.SemaphoreType.DMA((3, chunks, 2 * chips)),
        ],
        compiler_params=pltpu.CompilerParams(collective_id=0, has_side_effects=True, vmem_limit_bytes=48 << 20),
        name="mix",
    )(hidden, picked, gains, proj_w.T, w_gate.T, w_up.T, w_down)


def stats_kernel(n_keep, keep_tiles, head_ref, o_ref, *refs):
    keeps, (max_ref, sum_ref, slots, held, base, sems) = refs[:n_keep], refs[n_keep:]
    each = keep_tiles // n_keep
    vocab, tokens = head_ref.shape[0], o_ref.shape[1]
    full, tail = vocab // TILE, vocab % TILE
    depth = slots.shape[0]

    def fetch(tile, rows):
        slot = lax.rem(tile, depth)
        return pltpu.make_async_copy(
            head_ref.at[pl.ds(pl.multiple_of(tile * TILE, 16), rows), :],
            slots.at[slot, pl.ds(0, rows), :],
            sems.at[slot],
        )

    def fetch_any(tile):
        @pl.when(tile < full)
        def _():
            fetch(tile, TILE).start()

        if tail:

            @pl.when(tile == full)
            def _():
                fetch(tile, tail).start()

    def parts(rows):
        return [(top, min(HALF, rows - top)) for top in range(0, rows, HALF)]

    def groups(z):
        return z.reshape(z.shape[0] // 8, 8, z.shape[1])

    def rescale(lanes):
        top = max_ref[:, lanes]
        sum_ref[:, lanes] = sum_ref[:, lanes] * jnp.exp(base[:, lanes] - top)
        base[:, lanes] = top

    def add_held(top, size, lanes):
        z = groups(held[pl.ds(top, size), lanes])
        sum_ref[:, lanes] = sum_ref[:, lanes] + jnp.sum(jnp.exp(z - base[:, lanes][None]), axis=0)

    def work(tile, rows, keep):
        slot = lax.rem(tile, depth)
        for start in range(0, tokens, LANES):
            lanes = pl.ds(start, LANES)
            rescale(lanes)
            for top, size in parts(TILE):
                add_held(top, size, lanes)
                size = min(size, rows - top)
                z = jnp.dot(slots[slot, pl.ds(top, size), :], o_ref[:, lanes], preferred_element_type=F32)
                if keep is not None:
                    keeps[keep][pl.ds(pl.multiple_of((tile - keep * each) * TILE + top, 16), size), lanes] = z
                held[pl.ds(top, size), lanes] = z
                max_ref[:, lanes] = jnp.maximum(max_ref[:, lanes], jnp.max(groups(z), axis=0))

    for tile in range(depth - 1):
        fetch(tile, TILE).start()
    max_ref[...] = jnp.full_like(max_ref, LOWEST)
    base[...] = jnp.full_like(base, LOWEST)
    sum_ref[...] = jnp.zeros_like(sum_ref)
    held[...] = jnp.full_like(held, -jnp.inf)

    def step(keep, tile, carry):
        fetch_any(tile + depth - 1)
        fetch(tile, TILE).wait()
        work(tile, TILE, keep)
        return carry

    for index in range(n_keep):
        lax.fori_loop(index * each, (index + 1) * each, functools.partial(step, index), 0)
    lax.fori_loop(keep_tiles, full, functools.partial(step, None), 0)
    if tail:
        fetch(full, tail).wait()
        work(full, tail, None)
    for start in range(0, tokens, LANES):
        rescale(pl.ds(start, LANES))
        for top, size in parts(tail or TILE):
            add_held(top, size, pl.ds(start, LANES))


def head_stats(n_keep, keep_tiles, depth, head_t, o_t):
    vocab, dim = head_t.shape
    tokens = o_t.shape[1]
    vmem = pl.BlockSpec(memory_space=pltpu.VMEM)
    return pl.pallas_call(
        functools.partial(stats_kernel, n_keep, keep_tiles),
        out_shape=(*[pltpu.VMEM((keep_tiles // n_keep * TILE, tokens), F32)] * n_keep, jax.ShapeDtypeStruct((8, tokens), F32), jax.ShapeDtypeStruct((8, tokens), F32)),
        in_specs=[pl.BlockSpec(memory_space=pl.ANY), vmem],
        out_specs=(vmem,) * (n_keep + 2),
        scratch_shapes=[pltpu.VMEM((depth, TILE, dim), BF16), pltpu.VMEM((TILE, tokens), F32), pltpu.VMEM((8, tokens), F32), pltpu.SemaphoreType.DMA((depth,))],
        compiler_params=pltpu.CompilerParams(vmem_limit_bytes=12 << 20),
        name="head_stats",
    )(pltpu.with_memory_space_constraint(head_t, pltpu.HBM), o_t)

def merge_kernel(n_tp, max_ref, sum_ref, lse_ref, mine, theirs, send_sem, recv_sem):
    me = lax.axis_index("tp")
    barrier = pltpu.get_barrier_semaphore()
    for k in range(1, n_tp):
        peer = lax.rem(me + k, n_tp)
        pl.semaphore_signal(barrier, inc=1, device_id={"tp": peer}, device_id_type=MESH)
    tokens = max_ref.shape[1]
    top = jnp.max(max_ref[...], axis=0, keepdims=True)
    scaled = jnp.sum(sum_ref[...] * jnp.exp(max_ref[...] - top), axis=0, keepdims=True)
    mine[...] = jnp.concatenate([top, scaled], axis=0)
    pl.semaphore_wait(barrier, n_tp - 1)
    copies = []
    for k in range(1, n_tp):
        copy = pltpu.make_async_remote_copy(
            src_ref=mine,
            dst_ref=theirs.at[k - 1],
            send_sem=send_sem.at[k - 1],
            recv_sem=recv_sem.at[k - 1],
            device_id={"tp": lax.rem(me + k, n_tp)},
            device_id_type=MESH,
        )
        copy.start()
        copies.append(copy)
    for copy in copies:
        copy.wait()
    best, total = top, scaled
    for k in range(n_tp - 1):
        arrived = theirs[k]
        other, extra = arrived[0:1, :], arrived[1:2, :]
        new = jnp.maximum(best, other)
        total = total * jnp.exp(best - new) + extra * jnp.exp(other - new)
        best = new
    lse_ref[...] = jnp.broadcast_to(best + jnp.log(total), lse_ref.shape)


def merge(n_tp, maxima, sums):
    tokens = maxima.shape[1]
    vmem = pl.BlockSpec(memory_space=pltpu.VMEM)
    return pl.pallas_call(
        functools.partial(merge_kernel, n_tp),
        out_shape=jax.ShapeDtypeStruct((8, tokens), F32),
        in_specs=[vmem, vmem],
        out_specs=vmem,
        scratch_shapes=[
            pltpu.VMEM((2, tokens), F32),
            pltpu.VMEM((n_tp - 1, 2, tokens), F32),
            pltpu.SemaphoreType.DMA((n_tp - 1,)),
            pltpu.SemaphoreType.DMA((n_tp - 1,)),
        ],
        compiler_params=pltpu.CompilerParams(collective_id=1, has_side_effects=True, vmem_limit_bytes=2 << 20),
        name="merge",
    )(maxima, sums)


def logp_kernel(n_keep, keep_tiles, head_ref, o_ref, lse_ref, *refs):
    keeps = refs[:n_keep]
    out_ref, slots, made, kept, in_sems, made_sems, kept_sems = refs[n_keep:]
    vocab, tokens = head_ref.shape[0], o_ref.shape[1]
    each = keep_tiles // n_keep * 2
    kept_chunks = keep_tiles * 2
    base = keep_tiles * TILE
    rest = vocab - base
    steps, tail = rest // HALF, rest % HALF
    n_slots = kept.shape[0]
    spans = [steps * (i + 1) // n_keep for i in range(n_keep)]

    def fetch(step, rows):
        slot = lax.rem(step, 2)
        return pltpu.make_async_copy(
            head_ref.at[pl.ds(pl.multiple_of(base + step * HALF, 16), rows), :], slots.at[slot, pl.ds(0, rows), :], in_sems.at[slot])

    def put_made(step, rows):
        slot = lax.rem(step, 2)
        return pltpu.make_async_copy(
            made.at[slot, pl.ds(0, rows), :], out_ref.at[pl.ds(pl.multiple_of(base + step * HALF, 16), rows), :], made_sems.at[slot])

    def put_kept(chunk):
        slot = lax.rem(chunk, n_slots)
        return pltpu.make_async_copy(
            kept.at[slot], out_ref.at[pl.ds(pl.multiple_of(chunk * HALF, 16), HALF), :], kept_sems.at[slot])

    def do_kept(index, chunk):
        @pl.when(chunk >= n_slots)
        def _():
            put_kept(chunk - n_slots).wait()
        slot = lax.rem(chunk, n_slots)
        rows = pl.ds(pl.multiple_of((chunk - index * each) * HALF, 16), HALF)
        for start in range(0, tokens, LANES):
            lanes = pl.ds(start, LANES)
            kept[slot, :, lanes] = keeps[index][rows, lanes] - lse_ref[:, lanes][0:1, :]
        put_kept(chunk).start()

    def make(step, rows):
        slot = lax.rem(step, 2)
        for start in range(0, tokens, LANES):
            lanes = pl.ds(start, LANES)
            z = jnp.dot(slots[slot, pl.ds(0, rows), :], o_ref[:, lanes], preferred_element_type=F32)
            made[slot, pl.ds(0, rows), lanes] = z - lse_ref[:, lanes][0:1, :]

    def start_fetch(step):
        @pl.when(step < steps)
        def _():
            fetch(step, HALF).start()
        if tail:
            @pl.when(step == steps)
            def _():
                fetch(step, tail).start()

    start_fetch(0)
    done_steps = 0
    for index in range(n_keep):
        stop = spans[index]
        count = stop - done_steps
        per_step = each // count if count else 0

        def step_fn(step, carry, index=index, first=done_steps, per_step=per_step):
            start_fetch(step + 1)
            for i in range(per_step):
                do_kept(index, index * each + (step - first) * per_step + i)
            fetch(step, HALF).wait()
            @pl.when(step >= 2)
            def _():
                put_made(step - 2, HALF).wait()
            make(step, HALF)
            put_made(step, HALF).start()
            return carry

        lax.fori_loop(done_steps, stop, step_fn, 0)

        def kept_fn(chunk, carry, index=index):
            do_kept(index, chunk)
            return carry
        lax.fori_loop(index * each + count * per_step, (index + 1) * each, kept_fn, 0)
        done_steps = stop
    if tail:
        fetch(steps, tail).wait()
        put_made(steps - 2, HALF).wait()
        make(steps, tail)
        put_made(steps, tail).start()
        put_made(steps - 1, HALF).wait()
        put_made(steps, tail).wait()
    else:
        put_made(steps - 2, HALF).wait()
        put_made(steps - 1, HALF).wait()
    for i in range(n_slots):
        put_kept(kept_chunks - n_slots + i).wait()

def head_logp(n_keep, keep_tiles, n_kept, head_t, o_t, keeps, lse):
    vocab, dim = head_t.shape
    tokens = o_t.shape[1]
    vmem = pl.BlockSpec(memory_space=pltpu.VMEM)
    anym = pl.BlockSpec(memory_space=pl.ANY)
    return pl.pallas_call(
        functools.partial(logp_kernel, n_keep, keep_tiles),
        out_shape=jax.ShapeDtypeStruct((vocab, tokens), F32),
        in_specs=[anym] + [vmem] * (n_keep + 2),
        out_specs=anym,
        scratch_shapes=[
            pltpu.VMEM((2, HALF, dim), BF16),
            pltpu.VMEM((2, HALF, tokens), F32),
            pltpu.VMEM((n_kept, HALF, tokens), F32),
            pltpu.SemaphoreType.DMA((2,)), pltpu.SemaphoreType.DMA((2,)), pltpu.SemaphoreType.DMA((n_kept,)),
        ],
        compiler_params=pltpu.CompilerParams(vmem_limit_bytes=14 << 20),
        name="head_logp",
    )(pltpu.with_memory_space_constraint(head_t, pltpu.HBM), o_t, lse, *[pltpu.with_memory_space_constraint(keep, pltpu.VMEM) for keep in keeps])


def solution(mesh):
    n_tp = mesh.shape["tp"]

    def draft_step(hidden, tokens, embedding, head_w, h_norm, e_norm, f_norm, o_norm, proj_w, w_gate, w_up, w_down):
        vocab_local = embedding.shape[0]
        local_ids = tokens - lax.axis_index("tp") * vocab_local
        owned = (local_ids >= 0) & (local_ids < vocab_local)
        picked = gather_rows(embedding, local_ids, owned)
        gains = jnp.concatenate([h_norm, e_norm, f_norm, o_norm]).reshape(-1, 128)
        new_u, out_t = mix(n_tp, hidden, picked, gains, proj_w, w_gate, w_up, w_down)
        head_t = head_w.T
        *keeps, maxima, sums = head_stats(KEEPS, KEEP_TILES, 3, head_t, out_t)
        lse = merge(n_tp, maxima, sums)
        return new_u, head_logp(KEEPS, KEEP_TILES, 3, head_t, out_t, keeps, lse).T

    specs_in = (
        P("dp", None), P("dp"), P("tp", None), P(None, "tp"), P(None), P(None), P(None), P(None),
        P(None, "tp"), P(None, "tp"), P(None, "tp"), P("tp", None),
    )
    specs_out = (P("dp", None), P("dp", "tp"))
    return jax.shard_map(draft_step, mesh=mesh, in_specs=specs_in, out_specs=specs_out, check_vma=False)
```

time: 208 us -> 149 us (0.72); the launches traced: 206 us -> 149 us
  Pallas kernels: 198 us -> 143 us
    pallas_call x2, Pallas kernels: 99.6 us -> 59.4 us  [the longest x1 37.2 us: head_stats(): pl.pallas_call(functools.partial(stats_kernel, n_keep, keep_tiles), out_s...]
    pallas_call x1, Pallas kernels: 79.1 us -> 69.4 us  [mix(): pl.pallas_call(functools.partial(mix_kernel, n_tp), out_shape=(jax.ShapeD...]
    pallas_call x1, Pallas kernels: 9.95 us -> 5.31 us  [merge(): pl.pallas_call(functools.partial(merge_kernel, n_tp), out_shape=jax.Shape...]
    unnamed x21 -> x13, local copies, waits for them, and re-layouts: 5.45 us -> 3.51 us
where the time goes in v2:
time: 149 us
  Pallas kernels  143 us (96%)
  local copies, waits for them, and re-layouts  3.67 us (2%)
    pallas_call x1, Pallas kernels, mix(): pl.pallas_call(functools.partial(mix_kernel, n_tp), out_shape=(jax.ShapeD...  69.4 us
    pallas_call x1, Pallas kernels, head_stats(): pl.pallas_call(functools.partial(stats_kernel, n_keep, keep_tiles), out_s...  37.2 us
    pallas_call x1, Pallas kernels, head_logp(): pl.pallas_call(functools.partial(logp_kernel, n_keep, keep_tiles), out_sh...  22.1 us
    pallas_call x1, Pallas kernels, gather_rows(): pl.pallas_call(gather_kernel, out_shape=jax.ShapeDtypeStruct((rows, dim),...  9.04 us
    pallas_call x1, Pallas kernels, merge(): pl.pallas_call(functools.partial(merge_kernel, n_tp), out_shape=jax.Shape...  5.31 us
    unnamed x13, local copies, waits for them, and re-layouts  3.51 us

profile of v2, /device:TPU:113, one launch (start us, length us, event | category | flops | bytes accessed | tf_op | source)
XLA Modules:
  0.0 149.0 jit_solution(11282875545118267095)
XLA Ops:
  0.6 0.7 fusion.4
  1.3 0.7 pad_maximum_fusion.gains
  2.1 0.2 broadcast_in_dim.6.want_ref
  2.3 0.0 copy-start.2
  2.3 0.0 copy-start.3
  2.3 0.0 copy-start.4
  2.3 0.0 copy-start.5
  2.3 9.0 %gather_rows.1.picked_ref = bf16[768,896]{1,0:T(8,128)(2,1)S(1)} custom-call(s32[768]{0:T(1024)S(1)} %get-tuple-element.23.base_ref, s32[768,1]{1,0:T(8,128)S(1)} %broadcast_in_dim.6.want_ref, bf16[18992,896]{1,0:T(8,128)(2,1)} %table_ref.1), custom_call_target="tpu_custom_call" | custom-call | tf_op jit(solution)/shard_map/gather_rows/pallas_call | solution.py:60
  11.4 0.0 copy-start
  11.4 1.1 copy-done
  12.4 0.0 copy-done.2
  12.4 0.0 copy-done.3
  12.4 0.0 copy-done.4
  12.4 0.0 copy-done.5
  12.4 69.4 %mix.1 = (bf16[768,896]{1,0:T(8,128)(2,1)S(1)}, bf16[896,768]{1,0:T(8,128)(2,1)}) custom-call(bf16[768,896]{1,0:T(8,128)(2,1)} %hidden_ref.1, bf16[768,896]{1,0:T(8,128)(2,1)} %copy-done, f32[28,128]{1,0:T(8,128)S(1)} %pad_maximum_fusion.gains, bf16[112,1792]{1,0:T(8,128)(2,1)S(1)} %bitcast.11, bf16[608,896]{1,0:T(8,128)(2,1)S(1)} %bitcast.9, ...), custom_call_target="tpu_custom_call" | custom-call | tf_op jit(solution)/shard_map/mix/pallas_call | solution.py:298
  81.8 0.0 copy-start.1
  81.9 1.3 copy-done.1
  83.2 37.2 %head_stats.1 = (f32[2112,768]{1,0:T(8,128)S(1)}, f32[2112,768]{1,0:T(8,128)S(1)}, f32[2112,768]{1,0:T(8,128)S(1)}, f32[2112,768]{1,0:T(8,128)S(1)}, f32[2112,76...) custom-call(bf16[18992,896]{1,0:T(8,128)(2,1)} %bitcast.12, ...), custom_call_target="tpu_custom_call" | custom-call | tf_op jit(solution)/shard_map/head_stats/pallas_call | solution.py:410
  120.4 5.3 %merge.1.lse_ref = f32[8,768]{1,0:T(8,128)S(1)} custom-call(f32[8,768]{1,0:T(8,128)S(1)} %get-tuple-element.14.max_ref, f32[8,768]{1,0:T(8,128)S(1)} %get-tuple-element.15.sum_ref), custom_call_target="tpu_custom_call" | custom-call | tf_op jit(solution)/shard_map/merge/pallas_call | solution.py:458
  125.8 22.1 %head_logp.1 = f32[18992,768]{1,0:T(8,128)} custom-call(bf16[18992,896]{1,0:T(8,128)(2,1)} %bitcast.13, bf16[896,768]{1,0:T(8,128)(2,1)S(1)} %copy-done.1, f32[8,768]{1,0:T(8,128)S(1)} %merge.1.lse_ref, f32[2112,768]{1,0:T(8,128)S(1)} %get-tuple-element.16.refs_0_, f32[2112,768]{1,0:T(8,128)S(1)} %get-tuple-element.17.refs_1_, ...), custom_call_target="tpu_custom_call" | custom-call | tf_op jit(solution)/shard_map/head_logp/pallas_call | solution.py:572
  147.9 1.1 copy.16
Async XLA Ops:
  2.3 10.2 %copy-start.2 = (bf16[896,608]{0,1:T(8,128)(2,1)S(1)}, bf16[896,608]{0,1:T(8,128)(2,1)}, u32[]{:S(2)}) copy-start(bf16[896,608]{0,1:T(8,128)(2,1)} %param.21) | copy-start | bytes 3268612
  2.3 10.2 %copy-start.3 = (bf16[896,608]{0,1:T(8,128)(2,1)S(1)}, bf16[896,608]{0,1:T(8,128)(2,1)}, u32[]{:S(2)}) copy-start(bf16[896,608]{0,1:T(8,128)(2,1)} %param.22) | copy-start | bytes 3268612
  2.3 10.2 %copy-start.4 = (bf16[608,896]{1,0:T(8,128)(2,1)S(1)}, bf16[608,896]{1,0:T(8,128)(2,1)}, u32[]{:S(2)}) copy-start(bf16[608,896]{1,0:T(8,128)(2,1)} %down.1) | copy-start | bytes 3268612
  2.3 10.2 %copy-start.5 = (bf16[1792,112]{0,1:T(8,128)(2,1)S(1)}, bf16[1792,112]{0,1:T(8,128)(2,1)}, u32[]{:S(2)}) copy-start(bf16[1792,112]{0,1:T(8,128)(2,1)} %param.20) | copy-start | bytes 1204228
  11.4 1.1 copy-start
  81.8 1.3 copy-start.1

commit v3 on v2

--- a/solution.py
+++ b/solution.py
@@ -16,6 +16,7 @@
 KEEPS = 6
 KEEP_TILES = 12
 CHUNK = 256
+LAG = 0
 LOWEST = float(jnp.finfo(jnp.float32).min)
 F32 = jnp.float32
 BF16 = jnp.bfloat16
@@ -59,7 +60,7 @@
     want = jnp.where(owned, place * SLAB + ids % SLAB, -1)[:, None]
     return pl.pallas_call(
         gather_kernel,
-        out_shape=jax.ShapeDtypeStruct((rows, dim), BF16),
+        out_shape=pltpu.VMEM((rows, dim), BF16),
         in_specs=[
             pl.BlockSpec(memory_space=pltpu.SMEM),
             pl.BlockSpec(memory_space=pltpu.VMEM),
@@ -85,8 +86,8 @@
     return jnp.broadcast_to(gain, (128, gain.shape[1])).T
 
 
-def norm_columns(src_ref, dst_ref, gain):
-    gain = column_of(gain)
+def norm_columns(src_ref, dst_ref, gain_ref):
+    gain = gain_ref[...]
     dim, tokens = src_ref.shape
     for start in range(0, tokens, 128):
         lanes = pl.ds(start, 128)
@@ -111,6 +112,8 @@
     down,
     u_ref,
     o_ref,
+    columns,
+    down_t,
     h_normed,
     e_full,
     p_full,
@@ -119,9 +122,12 @@
     u_full,
     comb_e,
     pair_e,
+    half_e,
     far_e,
     part_d,
     pair_d,
+    comb_d,
+    half_d,
     far_d,
     send_rs,
     recv_rs,
@@ -138,13 +144,17 @@
     chunks = tokens // CHUNK
     t_rows = CHUNK // n_tp
     f_rows = proj_t.shape[0]
-    order = [2, 1, 3]
     contract_last = (((1,), (1,)), ((), ()))
-    contract_first = (((0,), (0,)), ((), ()))
 
     barrier = pltpu.get_barrier_semaphore()
     for peer in [partner] + [far[k] * 2 + core for k in range(1, chips)]:
         pl.semaphore_signal(barrier, inc=1, device_id={"tp": peer}, device_id_type=MESH)
+    for start in range(0, tokens, 64):
+        rows = pl.ds(start, 64)
+        h_normed[rows, :] = norm_rows(hidden_ref[rows, :].astype(F32), gain_row(gains, 0))
+    columns[0] = column_of(gain_row(gains, 2))
+    columns[1] = column_of(gain_row(gains, 3))
+    down_t[...] = down[...].T
     pl.semaphore_wait(barrier, chips)
 
     def push(src, dst, send_sem, recv_sem, device):
@@ -172,15 +182,54 @@
             for c in range(chips)
         ]
 
-    def far_send(src, landing, k, stage, chunk):
-        return push(
-            src, landing.at[chunk, k - 1], send_rs.at[stage, chunk, k], recv_rs.at[stage, chunk, k], far[k] * 2 + core
-        )
+    def halves(block):
+        rows, lanes = block
+        if isinstance(lanes, slice):
+            half = t_rows // 2
+            return [(pl.ds(pl.multiple_of(rows.start + half * side, 16), half), lanes) for side in range(2)]
+        half = CHUNK // 2
+        return [(rows, pl.ds(lanes.start + half * side, half)) for side in range(2)]
+
+    def neighbour_halves(shape):
+        if shape[0] == t_rows:
+            return [(pl.ds(t_rows // 2 * side, t_rows // 2), slice(None)) for side in range(2)]
+        return [(slice(None), pl.ds(CHUNK // 2 * side, CHUNK // 2)) for side in range(2)]
+
+    def across_send(sums, landing, stage, chunk):
+        parts = neighbour_halves(sums.shape[2:])
+        return [
+            push(
+                sums.at[(chunk, 2) + parts[side]],
+                landing.at[chunk, side],
+                send_rs.at[stage, chunk, side],
+                recv_rs.at[stage, chunk, side],
+                far[k] * 2 + core,
+            )
+            for side, k in ((0, 1), (1, 3))
+        ]
+
+    def next_send(sums, across, landing, into, stage, chunk):
+        parts = neighbour_halves(sums.shape[2:])
+        sends = []
+        for side, k in ((0, 1), (1, 3)):
+            across[side].wait()
+            view = (chunk, k) + parts[side]
+            sums[view] = sums[view] + landing[chunk, side]
+            sends.append(
+                push(
+                    sums.at[chunk, k],
+                    into.at[chunk, side],
+                    send_rs.at[stage, chunk, side],
+                    recv_rs.at[stage, chunk, side],
+                    far[k] * 2 + core,
+                )
+            )
+        return sends
 
     def gather_start(full, block, stage, chunk):
         own = full.at[block(me)]
         sends = {
-            k: push(own, own, send_ag.at[stage, chunk, k], recv_ag.at[stage, chunk, k], far[k] * 2 + core) for k in order
+            k: push(own, own, send_ag.at[stage, chunk, k], recv_ag.at[stage, chunk, k], far[k] * 2 + core) for k in (2, 1, 3)
         }
         near = push(own, own, send_ag.at[stage, chunk, 0], recv_ag.at[stage, chunk, 0], partner)
         return sends, near
@@ -208,26 +257,23 @@
     def e_start(chunk):
         live[chunk] = pair_send(picked_ref, token_block(chunk), pair_e, 0, chunk)
 
-    def h_norm(chunk):
-        for start in range(0, CHUNK, 64):
-            rows = pl.ds(chunk * CHUNK + start, 64)
-            h_normed[rows, :] = norm_rows(hidden_ref[rows, :].astype(F32), gain_row(gains, 0))
-
     def e_mid(chunk):
         for copy in live[chunk]:
             copy.wait()
-        block, sends = token_block(chunk), {}
-        for k in order + [0]:
+        block, across = token_block(chunk), None
+        for k in (2, 1, 3, 0):
             comb_e[chunk, k] = picked_ref[block(far[k] * 2 + core)] + pair_e[chunk, far[k]]
-            if k:
-                sends[k] = far_send(comb_e.at[chunk, k], far_e, k, 1, chunk)
-        live[chunk] = sends
+            across = across_send(comb_e, half_e, 1, chunk) if k == 2 else across
+        live[chunk] = across
+
+    def e_next(chunk):
+        live[chunk] = next_send(comb_e, live[chunk], half_e, far_e, 4, chunk)
 
     def e_end(chunk):
         total = comb_e[chunk, 0]
-        for k in [1, 3, 2]:
-            live[chunk][k].wait()
-            total = total + far_e[chunk, k - 1]
+        for side in range(2):
+            live[chunk][side].wait()
+            total = total + far_e[chunk, side]
         block = token_block(chunk)
         e_full[block(me)] = norm_rows(total.astype(F32), gain_row(gains, 1))
         live[chunk] = gather_start(e_full, block, 0, chunk)
@@ -249,28 +295,30 @@
     def feed_forward(chunk):
         gather_end(live[chunk])
         lanes = pl.ds(chunk * CHUNK, CHUNK)
-        norm_columns(p_full.at[:, lanes], n_full.at[:, lanes], gain_row(gains, 2))
+        norm_columns(p_full.at[:, lanes], n_full.at[:, lanes], columns.at[0])
         gate_val = jnp.dot(gate_t[...], n_full[:, lanes], preferred_element_type=F32)
         up_val = jnp.dot(up_t[...], n_full[:, lanes], preferred_element_type=F32)
         a_full[:, lanes] = (gate_val * jax.nn.sigmoid(gate_val) * up_val).astype(BF16)
-        part_d[:, lanes] = lax.dot_general(down[...], a_full[:, lanes], contract_first, preferred_element_type=F32)
+        part_d[:, lanes] = jnp.dot(down_t[...], a_full[:, lanes], preferred_element_type=F32)
         live[chunk] = pair_send(part_d, feature_block(chunk), pair_d, 2, chunk)
 
     def d_mid(chunk):
         for copy in live[chunk]:
             copy.wait()
-        block, sends = feature_block(chunk), {}
-        for k in order + [0]:
-            pair_d[chunk, far[k]] = part_d[block(far[k] * 2 + core)] + pair_d[chunk, far[k]]
-            if k:
-                sends[k] = far_send(pair_d.at[chunk, far[k]], far_d, k, 3, chunk)
-        live[chunk] = sends
+        block, across = feature_block(chunk), None
+        for k in (2, 1, 3, 0):
+            comb_d[chunk, k] = part_d[block(far[k] * 2 + core)] + pair_d[chunk, far[k]]
+            across = across_send(comb_d, half_d, 3, chunk) if k == 2 else across
+        live[chunk] = across
+
+    def d_next(chunk):
+        live[chunk] = next_send(comb_d, live[chunk], half_d, far_d, 5, chunk)
 
     def d_end(chunk):
-        summed = pair_d[chunk, chip]
-        for k in [1, 3, 2]:
-            live[chunk][k].wait()
-            summed = summed + far_d[chunk, k - 1]
+        summed = comb_d[chunk, 0]
+        for side in range(2):
+            live[chunk][side].wait()
+            summed = summed + far_d[chunk, side]
         block = feature_block(chunk)
         u_full[block(me)] = (p_full[block(me)].astype(F32) + summed).astype(BF16)
         live[chunk] = gather_start(u_full, block, 2, chunk)
@@ -281,13 +329,17 @@
     def finish(chunk):
         gather_end(live[chunk])
         lanes = pl.ds(chunk * CHUNK, CHUNK)
-        norm_columns(u_full.at[:, lanes], o_ref.at[:, lanes], gain_row(gains, 3))
+        norm_columns(u_full.at[:, lanes], o_ref.at[:, lanes], columns.at[1])
         for start in range(chunk * CHUNK, (chunk + 1) * CHUNK, 128):
             u_ref[pl.ds(start, 128), :] = u_full[:, pl.ds(start, 128)].T
 
-    for stage in (e_start, e_mid, h_norm, e_end, e_pass, project, p_pass, feed_forward, d_mid, d_end, u_pass, finish):
-        for chunk in range(chunks):
-            stage(chunk)
+    stages = (
+        e_start, e_mid, e_next, e_end, e_pass, project, p_pass, feed_forward,
+        d_mid, d_next, d_end, u_pass, finish,
+    )
+    turns = sorted((index + LAG * chunk, chunk, index) for index in range(len(stages)) for chunk in range(chunks))
+    for _, chunk, index in turns:
+        stages[index](chunk)
 
 
 def mix(n_tp, hidden, picked, gains, proj_w, w_gate, w_up, w_down):
@@ -297,10 +349,12 @@
     vmem = pl.BlockSpec(memory_space=pltpu.VMEM)
     return pl.pallas_call(
         functools.partial(mix_kernel, n_tp),
-        out_shape=(jax.ShapeDtypeStruct((tokens, dim), BF16), jax.ShapeDtypeStruct((dim, tokens), BF16)),
+        out_shape=(jax.ShapeDtypeStruct((tokens, dim), BF16), pltpu.VMEM((dim, tokens), BF16)),
         in_specs=[vmem] * 7,
         out_specs=(vmem, vmem),
         scratch_shapes=[
+            pltpu.VMEM((2, dim, 128), F32),
+            pltpu.VMEM((dim, ffn), BF16),
             pltpu.VMEM((tokens, dim), BF16),
             pltpu.VMEM((tokens, dim), BF16),
             pltpu.VMEM((dim, tokens), BF16),
@@ -309,22 +363,31 @@
             pltpu.VMEM((dim, tokens), BF16),
             pltpu.VMEM((chunks, chips, t_rows, dim), BF16),
             pltpu.VMEM((chunks, chips, t_rows, dim), BF16),
-            pltpu.VMEM((chunks, chips - 1, t_rows, dim), BF16),
+            pltpu.VMEM((chunks, 2, t_rows // 2, dim), BF16),
+            pltpu.VMEM((chunks, 2, t_rows, dim), BF16),
             pltpu.VMEM((dim, tokens), F32),
             pltpu.VMEM((chunks, chips, f_rows, CHUNK), F32),
-            pltpu.VMEM((chunks, chips - 1, f_rows, CHUNK), F32),
-            pltpu.SemaphoreType.DMA((4, chunks, chips)),
-            pltpu.SemaphoreType.DMA((4, chunks, chips)),
-            pltpu.SemaphoreType.DMA((3, chunks, 2 * chips)),
-            pltpu.SemaphoreType.DMA((3, chunks, 2 * chips)),
+            pltpu.VMEM((chunks, chips, f_rows, CHUNK), F32),
+            pltpu.VMEM((chunks, 2, f_rows, CHUNK // 2), F32),
+            pltpu.VMEM((chunks, 2, f_rows, CHUNK), F32),
+            pltpu.SemaphoreType.DMA((6, chunks, chips)),
+            pltpu.SemaphoreType.DMA((6, chunks, chips)),
+            pltpu.SemaphoreType.DMA((3, chunks, 10)),
+            pltpu.SemaphoreType.DMA((3, chunks, 10)),
         ],
-        compiler_params=pltpu.CompilerParams(collective_id=0, has_side_effects=True, vmem_limit_bytes=48 << 20),
+        compiler_params=pltpu.CompilerParams(collective_id=0, has_side_effects=True, vmem_limit_bytes=32 << 20),
         name="mix",
-    )(hidden, picked, gains, proj_w.T, w_gate.T, w_up.T, w_down)
-
-
-def stats_kernel(n_keep, keep_tiles, head_ref, o_ref, *refs):
-    keeps, (max_ref, sum_ref, slots, held, base, sems) = refs[:n_keep], refs[n_keep:]
+    )(*[pltpu.with_memory_space_constraint(x, pltpu.VMEM) for x in (hidden, picked, gains, proj_w.T, w_gate.T, w_up.T, w_down)])
+
+
+def stats_kernel(n_tp, n_keep, keep_tiles, head_ref, o_ref, lse_ref, *refs):
+    keeps = refs[:n_keep]
+    max_ref, sum_ref, slots, held, base, mine, theirs, sems, send_sem, recv_sem = refs[n_keep:]
+    me = lax.axis_index("tp")
+    peers = [lax.rem(me + k, n_tp) for k in range(1, n_tp)]
+    barrier = pltpu.get_barrier_semaphore()
+    for peer in peers:
+        pl.semaphore_signal(barrier, inc=1, device_id={"tp": peer}, device_id_type=MESH)
     each = keep_tiles // n_keep
     vocab, tokens = head_ref.shape[0], o_ref.shape[1]
     full, tail = vocab // TILE, vocab % TILE
@@ -402,48 +465,24 @@
         for top, size in parts(tail or TILE):
             add_held(top, size, pl.ds(start, LANES))
 
-
-def head_stats(n_keep, keep_tiles, depth, head_t, o_t):
-    vocab, dim = head_t.shape
-    tokens = o_t.shape[1]
-    vmem = pl.BlockSpec(memory_space=pltpu.VMEM)
-    return pl.pallas_call(
-        functools.partial(stats_kernel, n_keep, keep_tiles),
-        out_shape=(*[pltpu.VMEM((keep_tiles // n_keep * TILE, tokens), F32)] * n_keep, jax.ShapeDtypeStruct((8, tokens), F32), jax.ShapeDtypeStruct((8, tokens), F32)),
-        in_specs=[pl.BlockSpec(memory_space=pl.ANY), vmem],
-        out_specs=(vmem,) * (n_keep + 2),
-        scratch_shapes=[pltpu.VMEM((depth, TILE, dim), BF16), pltpu.VMEM((TILE, tokens), F32), pltpu.VMEM((8, tokens), F32), pltpu.SemaphoreType.DMA((depth,))],
-        compiler_params=pltpu.CompilerParams(vmem_limit_bytes=12 << 20),
-        name="head_stats",
-    )(pltpu.with_memory_space_constraint(head_t, pltpu.HBM), o_t)
-
-def merge_kernel(n_tp, max_ref, sum_ref, lse_ref, mine, theirs, send_sem, recv_sem):
-    me = lax.axis_index("tp")
-    barrier = pltpu.get_barrier_semaphore()
-    for k in range(1, n_tp):
-        peer = lax.rem(me + k, n_tp)
-        pl.semaphore_signal(barrier, inc=1, device_id={"tp": peer}, device_id_type=MESH)
-    tokens = max_ref.shape[1]
-    top = jnp.max(max_ref[...], axis=0, keepdims=True)
-    scaled = jnp.sum(sum_ref[...] * jnp.exp(max_ref[...] - top), axis=0, keepdims=True)
-    mine[...] = jnp.concatenate([top, scaled], axis=0)
+    best = jnp.max(max_ref[...], axis=0, keepdims=True)
+    total = jnp.sum(sum_ref[...] * jnp.exp(max_ref[...] - best), axis=0, keepdims=True)
+    mine[...] = jnp.concatenate([best, total], axis=0)
     pl.semaphore_wait(barrier, n_tp - 1)
     copies = []
-    for k in range(1, n_tp):
+    for k, peer in enumerate(peers):
         copy = pltpu.make_async_remote_copy(
             src_ref=mine,
-            dst_ref=theirs.at[k - 1],
-            send_sem=send_sem.at[k - 1],
-            recv_sem=recv_sem.at[k - 1],
-            device_id={"tp": lax.rem(me + k, n_tp)},
+            dst_ref=theirs.at[k],
+            send_sem=send_sem.at[k],
+            recv_sem=recv_sem.at[k],
+            device_id={"tp": peer},
             device_id_type=MESH,
         )
         copy.start()
         copies.append(copy)
-    for copy in copies:
+    for k, copy in enumerate(copies):
         copy.wait()
-    best, total = top, scaled
-    for k in range(n_tp - 1):
         arrived = theirs[k]
         other, extra = arrived[0:1, :], arrived[1:2, :]
         new = jnp.maximum(best, other)
@@ -452,23 +491,33 @@
     lse_ref[...] = jnp.broadcast_to(best + jnp.log(total), lse_ref.shape)
 
 
-def merge(n_tp, maxima, sums):
-    tokens = maxima.shape[1]
+def head_stats(n_tp, n_keep, keep_tiles, depth, head_t, o_t):
+    vocab, dim = head_t.shape
+    tokens = o_t.shape[1]
     vmem = pl.BlockSpec(memory_space=pltpu.VMEM)
     return pl.pallas_call(
-        functools.partial(merge_kernel, n_tp),
-        out_shape=jax.ShapeDtypeStruct((8, tokens), F32),
-        in_specs=[vmem, vmem],
-        out_specs=vmem,
+        functools.partial(stats_kernel, n_tp, n_keep, keep_tiles),
+        out_shape=(
+            jax.ShapeDtypeStruct((8, tokens), F32),
+            *[pltpu.VMEM((keep_tiles // n_keep * TILE, tokens), F32)] * n_keep,
+        ),
+        in_specs=[pl.BlockSpec(memory_space=pl.ANY), vmem],
+        out_specs=(vmem,) * (n_keep + 1),
         scratch_shapes=[
+            pltpu.VMEM((8, tokens), F32),
+            pltpu.VMEM((8, tokens), F32),
+            pltpu.VMEM((depth, TILE, dim), BF16),
+            pltpu.VMEM((TILE, tokens), F32),
+            pltpu.VMEM((8, tokens), F32),
             pltpu.VMEM((2, tokens), F32),
             pltpu.VMEM((n_tp - 1, 2, tokens), F32),
+            pltpu.SemaphoreType.DMA((depth,)),
             pltpu.SemaphoreType.DMA((n_tp - 1,)),
             pltpu.SemaphoreType.DMA((n_tp - 1,)),
         ],
-        compiler_params=pltpu.CompilerParams(collective_id=1, has_side_effects=True, vmem_limit_bytes=2 << 20),
-        name="merge",
-    )(maxima, sums)
+        compiler_params=pltpu.CompilerParams(collective_id=1, has_side_effects=True, vmem_limit_bytes=12 << 20),
+        name="head_stats",
+    )(pltpu.with_memory_space_constraint(head_t, pltpu.HBM), pltpu.with_memory_space_constraint(o_t, pltpu.VMEM))
 
 
 def logp_kernel(n_keep, keep_tiles, head_ref, o_ref, lse_ref, *refs):
@@ -582,7 +631,7 @@
         ],
         compiler_params=pltpu.CompilerParams(vmem_limit_bytes=14 << 20),
         name="head_logp",
-    )(pltpu.with_memory_space_constraint(head_t, pltpu.HBM), o_t, lse, *[pltpu.with_memory_space_constraint(keep, pltpu.VMEM) for keep in keeps])
+    )(pltpu.with_memory_space_constraint(head_t, pltpu.HBM), pltpu.with_memory_space_constraint(o_t, pltpu.VMEM), lse, *[pltpu.with_memory_space_constraint(keep, pltpu.VMEM) for keep in keeps])
 
 
 def solution(mesh):
@@ -596,8 +645,7 @@
         gains = jnp.concatenate([h_norm, e_norm, f_norm, o_norm]).reshape(-1, 128)
         new_u, out_t = mix(n_tp, hidden, picked, gains, proj_w, w_gate, w_up, w_down)
         head_t = head_w.T
-        *keeps, maxima, sums = head_stats(KEEPS, KEEP_TILES, 3, head_t, out_t)
-        lse = merge(n_tp, maxima, sums)
+        lse, *keeps = head_stats(n_tp, KEEPS, KEEP_TILES, 3, head_t, out_t)
         return new_u, head_logp(KEEPS, KEEP_TILES, 3, head_t, out_t, keeps, lse).T
 
     specs_in = (

time: 149 us -> 138 us (0.926)
  Pallas kernels: 143 us -> 134 us
  local copies, waits for them, and re-layouts: 3.67 us -> 1.27 us
    pallas_call x1, Pallas kernels: 69.4 us -> 61.6 us  [mix(): pl.pallas_call(functools.partial(mix_kernel, n_tp), out_shape=(jax.ShapeD...]
    unnamed x13 -> x11, local copies, waits for them, and re-layouts: 3.51 us -> 1.11 us
    pallas_call x3 -> x2, Pallas kernels: 51.6 us -> 50.2 us  [the longest x1 41.2 us: head_stats(): pl.pallas_call(functools.partial(stats_kernel, n_tp, n_keep, keep_tiles),...]
where the time goes in v3:
time: 138 us
  Pallas kernels  134 us (97%)
  other arithmetic  1.46 us (1%)
    pallas_call x1, Pallas kernels, mix(): pl.pallas_call(functools.partial(mix_kernel, n_tp), out_shape=(jax.ShapeD...  61.6 us
    pallas_call x1, Pallas kernels, head_stats(): pl.pallas_call(functools.partial(stats_kernel, n_tp, n_keep, keep_tiles),...  41.2 us
    pallas_call x1, Pallas kernels, head_logp(): pl.pallas_call(functools.partial(logp_kernel, n_keep, keep_tiles), out_sh...  22.2 us
    pallas_call x1, Pallas kernels, gather_rows(): pl.pallas_call(gather_kernel, out_shape=pltpu.VMEM((rows, dim), BF16), in...  9.04 us

profile of v3, /device:TPU:113, one launch (start us, length us, event | category | flops | bytes accessed | tf_op | source)
XLA Modules:
  0.0 137.5 jit_solution(3438485002172160739)
XLA Ops:
  0.6 0.7 fusion.4
  1.3 0.7 pad_maximum_fusion.gains
  2.1 0.2 broadcast_in_dim.6.want_ref
  2.3 0.0 copy-start
  2.3 0.0 copy-start.1
  2.3 0.0 copy-start.2
  2.3 0.0 copy-start.3
  2.3 0.0 copy-start.4
  2.3 9.0 %gather_rows.1.picked_ref = bf16[768,896]{1,0:T(8,128)(2,1)S(1)} custom-call(s32[768]{0:T(1024)S(1)} %get-tuple-element.21.base_ref, s32[768,1]{1,0:T(8,128)S(1)} %broadcast_in_dim.6.want_ref, bf16[18992,896]{1,0:T(8,128)(2,1)} %table_ref.1), custom_call_target="tpu_custom_call" | custom-call | tf_op jit(solution)/shard_map/gather_rows/pallas_call | solution.py:61
  11.4 0.0 copy-done
  11.4 0.0 copy-done.1
  11.4 0.0 copy-done.2
  11.4 0.0 copy-done.3
  11.4 0.0 copy-done.4
  11.4 61.6 %mix.1 = (bf16[768,896]{1,0:T(8,128)(2,1)S(1)}, bf16[896,768]{1,0:T(8,128)(2,1)S(1)}) custom-call(bf16[768,896]{1,0:T(8,128)(2,1)S(1)} %copy-done, bf16[768,896]{1,0:T(8,128)(2,1)S(1)} %gather_rows.1.picked_ref, f32[28,128]{1,0:T(8,128)S(1)} %pad_maximum_fusion.gains, bf16[112,1792]{1,0:T(8,128)(2,1)S(1)} %bitcast.11, bf16[608,896]{1,0:T(8,128)(2,1)S(1)} %bitcast.9, ...), custom_call_target="tpu_custom_call" | custom-call | tf_op jit(solution)/shard_map/mix/pallas_call | solution.py:350
  73.0 41.2 %head_stats.1 = (f32[8,768]{1,0:T(8,128)S(1)}, f32[2112,768]{1,0:T(8,128)S(1)}, f32[2112,768]{1,0:T(8,128)S(1)}, f32[2112,768]{1,0:T(8,128)S(1)}, f32[2112,768]{...) custom-call(bf16[18992,896]{1,0:T(8,128)(2,1)} %bitcast.12, bf16[896,768]{1,0:T(8,128)(2,1)S(1)} %get-tuple-element.12.o_ref), custom_call_target="tpu_custom_call" | custom-call | tf_op jit(solution)/shard_map/head_stats/pallas_call | solution.py:498
  114.3 22.2 %head_logp.1 = f32[18992,768]{1,0:T(8,128)} custom-call(bf16[18992,896]{1,0:T(8,128)(2,1)} %bitcast.13, bf16[896,768]{1,0:T(8,128)(2,1)S(1)} %get-tuple-element.12.o_ref, f32[8,768]{1,0:T(8,128)S(1)} %get-tuple-element.13.lse_ref, f32[2112,768]{1,0:T(8,128)S(1)} %get-tuple-element.14.refs_0_, f32[2112,768]{1,0:T(8,128)S(1)} %get-tuple-element.15.refs_1_, ...), custom_call_target="tpu_custom_call" | custom-call | tf_op jit(solution)/shard_map/head_logp/pallas_call | solution.py:621
  136.4 1.1 copy.16
Async XLA Ops:
  2.3 9.1 %copy-start = (bf16[768,896]{1,0:T(8,128)(2,1)S(1)}, bf16[768,896]{1,0:T(8,128)(2,1)}, u32[]{:S(2)}) copy-start(bf16[768,896]{1,0:T(8,128)(2,1)} %hidden_ref.1) | copy-start | bytes 4128772
  2.3 9.1 %copy-start.1 = (bf16[896,608]{0,1:T(8,128)(2,1)S(1)}, bf16[896,608]{0,1:T(8,128)(2,1)}, u32[]{:S(2)}) copy-start(bf16[896,608]{0,1:T(8,128)(2,1)} %param.21) | copy-start | bytes 3268612
  2.3 9.1 %copy-start.2 = (bf16[896,608]{0,1:T(8,128)(2,1)S(1)}, bf16[896,608]{0,1:T(8,128)(2,1)}, u32[]{:S(2)}) copy-start(bf16[896,608]{0,1:T(8,128)(2,1)} %param.22) | copy-start | bytes 3268612
  2.3 9.1 %copy-start.3 = (bf16[608,896]{1,0:T(8,128)(2,1)S(1)}, bf16[608,896]{1,0:T(8,128)(2,1)}, u32[]{:S(2)}) copy-start(bf16[608,896]{1,0:T(8,128)(2,1)} %down.1) | copy-start | bytes 3268612
  2.3 9.1 %copy-start.4 = (bf16[1792,112]{0,1:T(8,128)(2,1)S(1)}, bf16[1792,112]{0,1:T(8,128)(2,1)}, u32[]{:S(2)}) copy-start(bf16[1792,112]{0,1:T(8,128)(2,1)} %param.20) | copy-start | bytes 1204228

commit v4 on v3

--- a/solution.py
+++ b/solution.py
@@ -76,10 +76,9 @@
     )(ids // SLAB * SLAB, want, embedding)
 
 
-def gain_row(gains, index):
-    packed = gains[...]
-    count = packed.shape[0] // 4
-    return jnp.concatenate([packed[index * count + j : index * count + j + 1, :] for j in range(count)], axis=1)
+def gain_row(gain_ref):
+    packed = gain_ref[...]
+    return jnp.concatenate([packed[j : j + 1, :] for j in range(packed.shape[0])], axis=1)
 
 
 def column_of(gain):
@@ -105,12 +104,15 @@
     n_tp,
     hidden_ref,
     picked_ref,
-    gains,
+    h_gain,
+    e_gain,
+    f_gain,
+    o_gain,
     proj_t,
     gate_t,
     up_t,
     down,
-    u_ref,
+    u_full,
     o_ref,
     columns,
     down_t,
@@ -119,7 +121,6 @@
     p_full,
     n_full,
     a_full,
-    u_full,
     comb_e,
     pair_e,
     half_e,
@@ -151,9 +152,9 @@
         pl.semaphore_signal(barrier, inc=1, device_id={"tp": peer}, device_id_type=MESH)
     for start in range(0, tokens, 64):
         rows = pl.ds(start, 64)
-        h_normed[rows, :] = norm_rows(hidden_ref[rows, :].astype(F32), gain_row(gains, 0))
-    columns[0] = column_of(gain_row(gains, 2))
-    columns[1] = column_of(gain_row(gains, 3))
+        h_normed[rows, :] = norm_rows(hidden_ref[rows, :].astype(F32), gain_row(h_gain))
+    columns[0] = column_of(gain_row(f_gain))
+    columns[1] = column_of(gain_row(o_gain))
     down_t[...] = down[...].T
     pl.semaphore_wait(barrier, chips)
 
@@ -275,7 +276,7 @@
             live[chunk][side].wait()
             total = total + far_e[chunk, side]
         block = token_block(chunk)
-        e_full[block(me)] = norm_rows(total.astype(F32), gain_row(gains, 1))
+        e_full[block(me)] = norm_rows(total.astype(F32), gain_row(e_gain))
         live[chunk] = gather_start(e_full, block, 0, chunk)
 
     def e_pass(chunk):
@@ -330,8 +331,6 @@
         gather_end(live[chunk])
         lanes = pl.ds(chunk * CHUNK, CHUNK)
         norm_columns(u_full.at[:, lanes], o_ref.at[:, lanes], columns.at[1])
-        for start in range(chunk * CHUNK, (chunk + 1) * CHUNK, 128):
-            u_ref[pl.ds(start, 128), :] = u_full[:, pl.ds(start, 128)].T
 
     stages = (
         e_start, e_mid, e_next, e_end, e_pass, project, p_pass, feed_forward,
@@ -349,8 +348,8 @@
     vmem = pl.BlockSpec(memory_space=pltpu.VMEM)
     return pl.pallas_call(
         functools.partial(mix_kernel, n_tp),
-        out_shape=(jax.ShapeDtypeStruct((tokens, dim), BF16), pltpu.VMEM((dim, tokens), BF16)),
-        in_specs=[vmem] * 7,
+        out_shape=(pltpu.VMEM((dim, tokens), BF16), pltpu.VMEM((dim, tokens), BF16)),
+        in_specs=[vmem] * 10,
         out_specs=(vmem, vmem),
         scratch_shapes=[
             pltpu.VMEM((2, dim, 128), F32),
@@ -360,7 +359,6 @@
             pltpu.VMEM((dim, tokens), BF16),
             pltpu.VMEM((dim, tokens), BF16),
             pltpu.VMEM((ffn, tokens), BF16),
-            pltpu.VMEM((dim, tokens), BF16),
             pltpu.VMEM((chunks, chips, t_rows, dim), BF16),
             pltpu.VMEM((chunks, chips, t_rows, dim), BF16),
             pltpu.VMEM((chunks, 2, t_rows // 2, dim), BF16),
@@ -377,7 +375,7 @@
         ],
         compiler_params=pltpu.CompilerParams(collective_id=0, has_side_effects=True, vmem_limit_bytes=32 << 20),
         name="mix",
-    )(*[pltpu.with_memory_space_constraint(x, pltpu.VMEM) for x in (hidden, picked, gains, proj_w.T, w_gate.T, w_up.T, w_down)])
+    )(*[pltpu.with_memory_space_constraint(x, pltpu.VMEM) for x in (hidden, picked, *gains, proj_w.T, w_gate.T, w_up.T, w_down)])
 
 
 def stats_kernel(n_tp, n_keep, keep_tiles, head_ref, o_ref, lse_ref, *refs):
@@ -413,7 +411,7 @@
                 fetch(tile, tail).start()
 
     def parts(rows):
-        return [(top, min(HALF, rows - top)) for top in range(0, rows, HALF)]
+        return [(0, rows)]
 
     def groups(z):
         return z.reshape(z.shape[0] // 8, 8, z.shape[1])
@@ -520,9 +518,9 @@
     )(pltpu.with_memory_space_constraint(head_t, pltpu.HBM), pltpu.with_memory_space_constraint(o_t, pltpu.VMEM))
 
 
-def logp_kernel(n_keep, keep_tiles, head_ref, o_ref, lse_ref, *refs):
+def logp_kernel(n_keep, keep_tiles, head_ref, o_ref, u_t, lse_ref, *refs):
     keeps = refs[:n_keep]
-    out_ref, slots, made, kept, in_sems, made_sems, kept_sems = refs[n_keep:]
+    out_ref, u_ref, slots, made, kept, u_rows, in_sems, made_sems, kept_sems, u_sem = refs[n_keep:]
     vocab, tokens = head_ref.shape[0], o_ref.shape[1]
     each = keep_tiles // n_keep * 2
     kept_chunks = keep_tiles * 2
@@ -575,6 +573,7 @@
                 fetch(step, tail).start()
 
     start_fetch(0)
+    u_copy = pltpu.make_async_copy(u_rows, u_ref, u_sem)
     done_steps = 0
     for index in range(n_keep):
         stop = spans[index]
@@ -599,7 +598,11 @@
             do_kept(index, chunk)
             return carry
         lax.fori_loop(index * each + count * per_step, (index + 1) * each, kept_fn, 0)
+        if index < tokens // 256:
+            for start in range(index * 256, (index + 1) * 256, 128):
+                u_rows[pl.ds(start, 128), :] = u_t[:, pl.ds(start, 128)].T
         done_steps = stop
+    u_copy.start()
     if tail:
         fetch(steps, tail).wait()
         put_made(steps - 2, HALF).wait()
@@ -612,26 +615,28 @@
         put_made(steps - 1, HALF).wait()
     for i in range(n_slots):
         put_kept(kept_chunks - n_slots + i).wait()
-
-def head_logp(n_keep, keep_tiles, n_kept, head_t, o_t, keeps, lse):
+    u_copy.wait()
+
+def head_logp(n_keep, keep_tiles, n_kept, head_t, o_t, u_t, keeps, lse):
     vocab, dim = head_t.shape
     tokens = o_t.shape[1]
     vmem = pl.BlockSpec(memory_space=pltpu.VMEM)
     anym = pl.BlockSpec(memory_space=pl.ANY)
     return pl.pallas_call(
         functools.partial(logp_kernel, n_keep, keep_tiles),
-        out_shape=jax.ShapeDtypeStruct((vocab, tokens), F32),
-        in_specs=[anym] + [vmem] * (n_keep + 2),
-        out_specs=anym,
+        out_shape=(jax.ShapeDtypeStruct((vocab, tokens), F32), jax.ShapeDtypeStruct((tokens, dim), BF16)),
+        in_specs=[anym] + [vmem] * (n_keep + 3),
+        out_specs=(anym, anym),
         scratch_shapes=[
             pltpu.VMEM((2, HALF, dim), BF16),
             pltpu.VMEM((2, HALF, tokens), F32),
             pltpu.VMEM((n_kept, HALF, tokens), F32),
-            pltpu.SemaphoreType.DMA((2,)), pltpu.SemaphoreType.DMA((2,)), pltpu.SemaphoreType.DMA((n_kept,)),
+            pltpu.VMEM((tokens, dim), BF16),
+            pltpu.SemaphoreType.DMA((2,)), pltpu.SemaphoreType.DMA((2,)), pltpu.SemaphoreType.DMA((n_kept,)), pltpu.SemaphoreType.DMA,
         ],
-        compiler_params=pltpu.CompilerParams(vmem_limit_bytes=14 << 20),
+        compiler_params=pltpu.CompilerParams(vmem_limit_bytes=16 << 20),
         name="head_logp",
-    )(pltpu.with_memory_space_constraint(head_t, pltpu.HBM), pltpu.with_memory_space_constraint(o_t, pltpu.VMEM), lse, *[pltpu.with_memory_space_constraint(keep, pltpu.VMEM) for keep in keeps])
+    )(pltpu.with_memory_space_constraint(head_t, pltpu.HBM), pltpu.with_memory_space_constraint(o_t, pltpu.VMEM), pltpu.with_memory_space_constraint(u_t, pltpu.VMEM), lse, *[pltpu.with_memory_space_constraint(keep, pltpu.VMEM) for keep in keeps])
 
 
 def solution(mesh):
@@ -642,11 +647,12 @@
         local_ids = tokens - lax.axis_index("tp") * vocab_local
         owned = (local_ids >= 0) & (local_ids < vocab_local)
         picked = gather_rows(embedding, local_ids, owned)
-        gains = jnp.concatenate([h_norm, e_norm, f_norm, o_norm]).reshape(-1, 128)
-        new_u, out_t = mix(n_tp, hidden, picked, gains, proj_w, w_gate, w_up, w_down)
+        gains = [gain.reshape(-1, 128) for gain in (h_norm, e_norm, f_norm, o_norm)]
+        u_t, out_t = mix(n_tp, hidden, picked, gains, proj_w, w_gate, w_up, w_down)
         head_t = head_w.T
         lse, *keeps = head_stats(n_tp, KEEPS, KEEP_TILES, 3, head_t, out_t)
-        return new_u, head_logp(KEEPS, KEEP_TILES, 3, head_t, out_t, keeps, lse).T
+        logp_t, new_u = head_logp(KEEPS, KEEP_TILES, 3, head_t, out_t, u_t, keeps, lse)
+        return new_u, logp_t.T
 
     specs_in = (
         P("dp", None), P("dp"), P("tp", None), P(None, "tp"), P(None), P(None), P(None), P(None),

time: 138 us -> 137 us (level)
  no operation moved by 1% of the time
where the time goes in v4:
time: 137 us; the launch traced here: 136 us
  Pallas kernels  134 us (98%)
    pallas_call x1, Pallas kernels, mix(): pl.pallas_call(functools.partial(mix_kernel, n_tp), out_shape=(pltpu.VMEM...  61.5 us
    pallas_call x1, Pallas kernels, head_stats(): pl.pallas_call(functools.partial(stats_kernel, n_tp, n_keep, keep_tiles),...  40.3 us
    pallas_call x1, Pallas kernels, head_logp(): pl.pallas_call(functools.partial(logp_kernel, n_keep, keep_tiles), out_sh...  23 us
    pallas_call x1, Pallas kernels, gather_rows(): pl.pallas_call(gather_kernel, out_shape=pltpu.VMEM((rows, dim), BF16), in...  9.04 us

profile of v4, /device:TPU:113, one launch (start us, length us, event | category | flops | bytes accessed | tf_op | source)
XLA Modules:
  0.0 136.4 jit_solution(1345862036710502977)
XLA Ops:
  0.6 0.7 fusion.4
  1.3 0.2 broadcast_in_dim.6.want_ref
  1.5 0.0 copy-start
  1.5 0.0 copy-start.1
  1.5 0.0 copy-start.2
  1.5 0.0 copy-start.3
  1.6 0.0 copy-start.4
  1.6 0.0 copy-start.6
  1.6 0.0 copy-start.7
  1.6 0.0 copy-start.8
  1.6 0.0 copy-start.9
  1.6 9.0 %gather_rows.1.picked_ref = bf16[768,896]{1,0:T(8,128)(2,1)S(1)} custom-call(s32[768]{0:T(1024)S(1)} %get-tuple-element.25.base_ref, s32[768,1]{1,0:T(8,128)S(1)} %broadcast_in_dim.6.want_ref, bf16[18992,896]{1,0:T(8,128)(2,1)} %table_ref.1), custom_call_target="tpu_custom_call" | custom-call | tf_op jit(solution)/shard_map/gather_rows/pallas_call | solution.py:61
  10.7 0.0 copy-done
  10.7 0.0 copy-done.1
  10.7 0.0 copy-done.2
  10.7 0.0 copy-done.3
  10.7 0.0 copy-done.4
  10.7 0.0 copy-done.6
  10.7 0.0 copy-done.7
  10.7 0.0 copy-done.8
  10.7 0.0 copy-done.9
  10.8 61.5 %mix.1 = (bf16[896,768]{1,0:T(8,128)(2,1)S(1)}, bf16[896,768]{1,0:T(8,128)(2,1)S(1)}) custom-call(bf16[768,896]{1,0:T(8,128)(2,1)S(1)} %copy-done, bf16[768,896]{1,0:T(8,128)(2,1)S(1)} %gather_rows.1.picked_ref, f32[7,128]{1,0:T(8,128)S(1)} %bitcast.12, f32[7,128]{1,0:T(8,128)S(1)} %bitcast.13, f32[7,128]{1,0:T(8,128)S(1)} %bitcast.14, ...), custom_call_target="tpu_custom_call" | custom-call | tf_op jit(solution)/shard_map/mix/pallas_call | solution.py:349
  72.3 40.3 %head_stats.1 = (f32[8,768]{1,0:T(8,128)S(1)}, f32[2112,768]{1,0:T(8,128)S(1)}, f32[2112,768]{1,0:T(8,128)S(1)}, f32[2112,768]{1,0:T(8,128)S(1)}, f32[2112,768]{...) custom-call(bf16[18992,896]{1,0:T(8,128)(2,1)} %bitcast.16, bf16[896,768]{1,0:T(8,128)(2,1)S(1)} %get-tuple-element.13.o_ref), custom_call_target="tpu_custom_call" | custom-call | tf_op jit(solution)/shard_map/head_stats/pallas_call | solution.py:496
  112.6 0.0 copy-start.5
  112.6 0.6 copy-done.5
  113.2 23.0 %head_logp.1 = (f32[18992,768]{1,0:T(8,128)}, bf16[768,896]{1,0:T(8,128)(2,1)}) custom-call(bf16[18992,896]{1,0:T(8,128)(2,1)} %bitcast.17, bf16[896,768]{1,0:T(8,128)(2,1)S(1)} %get-tuple-element.13.o_ref, bf16[896,768]{1,0:T(8,128)(2,1)S(1)} %get-tuple-element.14.u_t, f32[8,768]{1,0:T(8,128)} %copy-done.5, f32[2112,768]{1,0:T(8,128)S(1)} %get-tuple-element.16.refs_0_, ...), custom_call_target="tpu_custom_call" | custom-call | tf_op jit(solution)/shard_map/head_logp/pallas_call | solution.py:625
Async XLA Ops:
  1.5 9.2 %copy-start = (bf16[768,896]{1,0:T(8,128)(2,1)S(1)}, bf16[768,896]{1,0:T(8,128)(2,1)}, u32[]{:S(2)}) copy-start(bf16[768,896]{1,0:T(8,128)(2,1)} %hidden_ref.1) | copy-start | bytes 4128772
  1.5 9.2 %copy-start.1 = (bf16[896,608]{0,1:T(8,128)(2,1)S(1)}, bf16[896,608]{0,1:T(8,128)(2,1)}, u32[]{:S(2)}) copy-start(bf16[896,608]{0,1:T(8,128)(2,1)} %param.21) | copy-start | bytes 3268612
  1.5 9.2 %copy-start.2 = (bf16[896,608]{0,1:T(8,128)(2,1)S(1)}, bf16[896,608]{0,1:T(8,128)(2,1)}, u32[]{:S(2)}) copy-start(bf16[896,608]{0,1:T(8,128)(2,1)} %param.22) | copy-start | bytes 3268612
  1.5 9.2 %copy-start.3 = (bf16[608,896]{1,0:T(8,128)(2,1)S(1)}, bf16[608,896]{1,0:T(8,128)(2,1)}, u32[]{:S(2)}) copy-start(bf16[608,896]{1,0:T(8,128)(2,1)} %down.1) | copy-start | bytes 3268612
  1.6 9.2 %copy-start.4 = (bf16[1792,112]{0,1:T(8,128)(2,1)S(1)}, bf16[1792,112]{0,1:T(8,128)(2,1)}, u32[]{:S(2)}) copy-start(bf16[1792,112]{0,1:T(8,128)(2,1)} %param.20) | copy-start | bytes 1204228
  1.6 9.1 %copy-start.6 = (f32[896]{0:T(1024)S(1)}, f32[896]{0:T(1024)}, u32[]{:S(2)}) copy-start(f32[896]{0:T(1024)} %param.16) | copy-start | bytes 10756
  1.6 9.1 %copy-start.7 = (f32[896]{0:T(1024)S(1)}, f32[896]{0:T(1024)}, u32[]{:S(2)}) copy-start(f32[896]{0:T(1024)} %param.17) | copy-start | bytes 10756
  1.6 9.1 %copy-start.8 = (f32[896]{0:T(1024)S(1)}, f32[896]{0:T(1024)}, u32[]{:S(2)}) copy-start(f32[896]{0:T(1024)} %param.18) | copy-start | bytes 10756
  1.6 9.1 %copy-start.9 = (f32[896]{0:T(1024)S(1)}, f32[896]{0:T(1024)}, u32[]{:S(2)}) copy-start(f32[896]{0:T(1024)} %param.19) | copy-start | bytes 10756
  112.6 0.6 copy-start.5
